TPU v7x, 256 devices: a whole 4x4x8 slice. The times are simulated.
256 devices in a mesh: freq: 64 (over x, z, core), kgrp: 4 (over y).
Axes of the slice: x: 4, y: 4, z: 8, core: 2. Of those that a mesh axis runs over, the one named last changes fastest.
Arguments:
- hamiltonian: float32 [256, 64, 128], P(('freq', 'kgrp')), may hold values from -1 to 1, as said below
- self_energy: float32 [128, 64, 128], P('freq'), may hold values from -0.8 to 0.3, as said below
- guess_factor: float32 [128, 64, 128], P('freq'), may hold values from -0.05 to 1.25
- weights: int32 [256], replicated, may hold values from 1 to 48
- counts: int32 [128], replicated, may hold values from 1 to 3, as said below
Outputs:
- local_green: float32 [4096, 256], P(('freq', 'kgrp'))
Inputs may be any that keep to these rules, and one draw needn't show every extreme that they name: `hamiltonian`: each k-point's matrix is Hermitian: the left half symmetric, the right half antisymmetric. `self_energy`: the diagonal of the right half lies between -0.8 and -0.4. `counts`: the number of Newton-Schulz steps taken at each frequency.
All inputs are finite; a program needn't handle non-finite values.
Results may differ from a plain program's by a relative error of at most 0.0001.
Values sent between devices are 32-bit elements.
A program may use at most 64 MiB of HBM per device.

v0:
```python
import math

import jax
import jax.numpy as jnp
from jax import lax
from jax.sharding import PartitionSpec as P

chem_potential = 0.2


def copy_for_each(value, axis):
    size = lax.axis_size(axis)
    return lax.all_to_all(
        jnp.broadcast_to(value[None], (size, *value.shape)), axis, 0, 0, tiled=True
    )


def in_order(pieces, dim):
    shape = list(pieces.shape[1:])
    shape[dim] *= pieces.shape[0]
    return jnp.moveaxis(pieces, 0, dim).reshape(shape)


def gather_directly(value, axis, dim):
    pieces = copy_for_each(value, axis)
    return in_order(pieces, dim)


def split_up(value, dim, size):
    shape = value.shape
    pieces = value.reshape(*shape[:dim], size, shape[dim] // size, *shape[dim + 1 :])
    return jnp.moveaxis(pieces, dim, 0)


def summed_on_arrival(value, axis, dim):
    pieces = split_up(value, dim, lax.axis_size(axis))
    arrived = lax.all_to_all(pieces, axis, split_axis=0, concat_axis=0, tiled=True)
    return arrived.sum(axis=0)


def blockify(right_side):
    order = right_side.shape[-1] // 2
    real_part = right_side[..., :order]
    imag_part = right_side[..., order:]
    upper_row = jnp.concatenate([real_part, imag_part], -1)
    lower_row = jnp.concatenate([-imag_part, real_part], -1)
    return jnp.concatenate([upper_row, lower_row], -2)


def complex_product(left_side, right_side):
    return jnp.einsum(
        "...ij,...jl->...il", left_side, blockify(right_side), precision=lax.Precision.HIGHEST
    )


def build_matrix(kpoint_rows, sigma_rows, matsubara):
    orbitals = kpoint_rows.shape[1]
    identity = jnp.eye(orbitals, dtype=jnp.float32)
    real_shift = jnp.broadcast_to(chem_potential * identity, matsubara.shape + identity.shape)
    imag_shift = matsubara[:, None, None] * identity
    diagonal_shift = jnp.concatenate([real_shift, imag_shift], -1)
    return diagonal_shift[:, None] - kpoint_rows[None] - sigma_rows[:, None]


def start_guess(matrix, factor_rows):
    orbitals = matrix.shape[-2]
    diag_real = jnp.diagonal(matrix[..., :orbitals], axis1=-2, axis2=-1)
    diag_imag = jnp.diagonal(matrix[..., orbitals:], axis1=-2, axis2=-1)
    modulus = diag_real * diag_real + diag_imag * diag_imag
    recip_real = (diag_real / modulus)[..., None]
    recip_imag = (-diag_imag / modulus)[..., None]
    factor_real = factor_rows[..., :orbitals]
    factor_imag = factor_rows[..., orbitals:]
    guess_real = recip_real * factor_real - recip_imag * factor_imag
    guess_imag = recip_real * factor_imag + recip_imag * factor_real
    return jnp.concatenate([guess_real, guess_imag], -1)


def invert_blocks(kpoint_rows, sigma_rows, factor_rows, freq_ids, freq_total, step_counts):
    orbitals = kpoint_rows.shape[1]
    matsubara = (2 * freq_ids + 1).astype(jnp.float32) * (math.pi / (2 * freq_total))
    matrix = build_matrix(kpoint_rows, sigma_rows, matsubara)
    initial = start_guess(matrix, factor_rows[:, None])
    identity = jnp.eye(orbitals, dtype=jnp.float32)
    doubled = jnp.concatenate([2.0 * identity, jnp.zeros_like(identity)], -1)
    longest = jnp.max(step_counts)

    def newton_step(sweep, current):
        updated = complex_product(current, doubled - complex_product(matrix, current))
        active = (sweep < step_counts)[:, None, None, None]
        return jnp.where(active, updated, current)

    return lax.fori_loop(0, longest, newton_step, initial)


def per_device(hamiltonian, self_energy, guess_factor, weights, counts):
    orbitals = hamiltonian.shape[1]
    per_freq = self_energy.shape[0]
    k_local = hamiltonian.shape[0]
    freq_devs = lax.axis_size("freq")
    group_devs = lax.axis_size("kgrp")
    freq_total = per_freq * freq_devs
    pair_block = orbitals * orbitals // (freq_devs * group_devs)
    freq_pos = lax.axis_index("freq")
    group_pos = lax.axis_index("kgrp")
    weight_total = jnp.sum(weights.astype(jnp.float32))
    first_freq = freq_pos * per_freq
    freq_ids = first_freq + jnp.arange(per_freq, dtype=jnp.int32)
    local_counts = lax.dynamic_slice_in_dim(counts, first_freq, per_freq)
    empty = jnp.zeros((per_freq, orbitals, 2 * orbitals), jnp.float32)
    h_piece = gather_directly(hamiltonian, "freq", 0)
    row_ids = jnp.arange(h_piece.shape[0], dtype=jnp.int32)
    kpoint_ids = (
        row_ids // k_local * (group_devs * k_local) + group_pos * k_local + row_ids % k_local
    )
    factors = jnp.take(weights, kpoint_ids).astype(jnp.float32)
    inverses = invert_blocks(h_piece, self_energy, guess_factor, freq_ids, freq_total, local_counts)
    partial_sum = empty + jnp.einsum(
        "k,fkij->fij", factors, inverses, precision=lax.Precision.HIGHEST
    )
    partial_term = partial_sum.reshape(per_freq, orbitals, 2, orbitals).transpose(0, 2, 1, 3)
    partial_term = partial_term.reshape(per_freq, 2, freq_devs, group_devs, pair_block)
    quarter = summed_on_arrival(partial_term, "kgrp", 3)
    own_block = lax.all_to_all(quarter, "freq", split_axis=2, concat_axis=0, tiled=True)
    result = own_block.reshape(freq_total, 2, pair_block).transpose(2, 1, 0)
    result = result.reshape(pair_block, 2 * freq_total)
    return result / weight_total


def solution(mesh):
    return jax.shard_map(
        per_device,
        mesh=mesh,
        in_specs=(
            P(("freq", "kgrp"), None, None),
            P("freq", None, None),
            P("freq", None, None),
            P(),
            P(),
        ),
        out_specs=P(("freq", "kgrp"), None),
        check_vma=False,
    )
```

profile of v0, /device:TPU:1, one launch (start us, length us, event | category | flops | bytes accessed | tf_op | source)
XLA Modules:
  0.0 248.0 jit_solution(15725272976597530600)
XLA Ops:
  0.0 2.3 broadcast_in_dim.46
  2.3 0.0 copy-start.1
  2.3 13.1 %all-to-all-start = ((f32[64,1,64,128]{3,2,1,0:T(8,128)}), f32[64,1,64,128]{3,2,1,0:T(8,128)S(1)}, u32[]{:S(2)}, u32[]{:S(2)}) async-start(f32[64,1,64,128]{3,2,1,0:T(8,128)} %broadcast_in_dim.46), calls=%async_computation | async-start | bytes 4194304 | tf_op jit(solution)/shard_map/all_to_all | solution.py:13
  15.5 0.1 broadcast_multiply_fusion
  15.6 0.1 pad_maximum_fusion.1
  15.7 0.0 copy-start
  15.7 0.0 copy-start.3
  15.7 0.0 copy-start.2
  15.7 2.6 %copy.22 = f32[2,64,128]{0,2,1:T(8,128)} copy(f32[2,64,128]{2,1,0:T(8,128)S(1)} %pad_maximum_fusion.1) | data formatting | bytes 131072 | tf_op jit(solution)/shard_map/concatenate | solution.py:61
  18.3 0.0 copy-done.1
  18.3 2.6 %copy.24 = f32[2,64,128]{0,2,1:T(8,128)} copy(f32[2,64,128]{2,1,0:T(8,128)S(1)} %copy-done.1) | data formatting | bytes 131072 | tf_op args[1]
  21.0 0.0 copy-done
  21.0 0.8 gather_fusion
  21.8 0.0 copy-done.3
  21.8 0.7 fusion.48
  22.5 0.0 copy-done.2
  22.5 0.1 slice_bitcast_fusion.1
  22.5 44.1 %all-to-all-done = f32[64,1,64,128]{3,2,1,0:T(8,128)S(1)} async-done(((f32[64,1,64,128]{3,2,1,0:T(8,128)}), f32[64,1,64,128]{3,2,1,0:T(8,128)S(1)}, u32[]{:S(2)}, u32[]{:S(2)}) %all-to-all-start) | async-done | bytes 2097184 | tf_op jit(solution)/shard_map/all_to_all | solution.py:13
  66.7 2.7 %copy.23 = f32[64,64,128]{0,2,1:T(8,128)} copy(f32[64,64,128]{2,1,0:T(8,128)S(1)} %bitcast.71) | data formatting | bytes 4194304 | tf_op jit(solution)/shard_map/sub | solution.py:62
  69.4 22.3 %subtract_subtract_fusion = f32[2,64,64,128]{1,0,3,2:T(2,128)} fusion(f32[2,64,128]{0,2,1:T(8,128)} %copy.24, f32[64,64,128]{0,2,1:T(8,128)} %copy.23, f32[2,64,128]{0,2,1:T(8,128)} %copy.22), kind=kLoop, calls=%fused_computation.30 | loop fusion | flops 2097152 | bytes 6422528 | tf_op jit(solution)/shard_map/sub | solution.py:62
  91.7 7.8 %fusion.49 = (f32[2,64,64,64]{1,0,3,2:T(2,128)}, f32[2,64,64,64]{1,0,3,2:T(2,128)}) fusion(f32[2,64,64,128]{1,0,3,2:T(2,128)} %subtract_subtract_fusion), kind=kLoop, calls=%fused_computation.71 | loop fusion | bytes 8388608 | tf_op jit(solution)/shard_map/slice | solution.py:67
  99.5 2.9 %gather_fusion.1 = f32[64,2,64]{2,1,0:T(2,128)S(1)} fusion(f32[2,64,64,64]{1,0,3,2:T(2,128)} %get-tuple-element.83, s32[64]{0:T(128)S(1)} %or_bitcast_fusion), kind=kCustom, calls=%fused_computation.1 | custom fusion | bytes 66048 | tf_op jit(solution)/shard_map/jit(diagonal)/gather | solution.py:67
  102.5 0.1 copy.25
  102.5 3.0 %gather_fusion.2 = f32[64,2,64]{2,1,0:T(2,128)S(1)} fusion(f32[2,64,64,64]{1,0,3,2:T(2,128)} %get-tuple-element.84, s32[64]{0:T(128)S(1)} %or_bitcast_fusion), kind=kCustom, calls=%fused_computation.2 | custom fusion | bytes 66048 | tf_op jit(solution)/shard_map/jit(diagonal)/gather | solution.py:68
  105.5 0.1 copy.26
  105.6 2.3 multiply_subtract_fusion
  107.9 3.1 %pad_maximum_fusion = f32[2,64,64,128]{3,2,1,0:T(8,128)} fusion(f32[2,64,64,64]{3,2,1,0:T(8,128)S(1)} %get-tuple-element.86, f32[2,64,64,64]{3,2,1,0:T(8,128)S(1)} %get-tuple-element.85), kind=kLoop, calls=%fused_computation.31 | loop fusion | flops 1048576 | bytes 8388608 | tf_op jit(solution)/shard_map/concatenate | solution.py:76
  111.0 86.8 %while.11 = (s32[]{:T(128)}, f32[2,64,64,128]{3,2,1,0:T(8,128)}, s32[]{:T(128)}, s32[2]{0:T(128)S(1)}, f32[64,128]{1,0:T(8,128)S(1)}, /*index=5*/f32[64,64,128]{...) while((s32[]{:T(128)}, f32[2,64,64,128]{3,2,1,0:T(8,128)}, ...), condition=%wide.region_2.3_spmd.clone, body=%wide.region_1.2_spmd.clone.sunk | while | flops 3234856960 | bytes 56787048 | solution.py:93
  111.8 2.2 copy.51
  114.0 1.4 slice_negate_fusion.4
  115.4 9.0 %bitcast_subtract_fusion.2 = f32[2,64,64,128]{3,2,1,0:T(8,128)S(1)} fusion(f32[64,128]{1,0:T(8,128)S(1)} %get-tuple-element.171, f32[2,64,128]{2,1,0:T(8,128)S(1)} %get-tuple-element.174, f32[64,64,128]{2,1,0:T(8,128)S(1)} %get-tuple-element.172, f32[2,64,128]{2,1,0:T(8,128)S(1)} %get-tuple-element.173, ...), kind=kOutput, calls=%fused_computation.18.clone.1 | convolution fusion | flops 1617952768 | bytes 14843904 | tf_op jit(solution)/shard_map/while/body/...ij,...jl->...il/dot_general | solution.py:51
  124.4 3.5 %slice_negate_fusion.5 = (f32[2,64,64,64]{3,2,1,0:T(8,128)S(1)}, f32[2,64,64,64]{3,2,1,0:T(8,128)}) fusion(f32[2,64,64,128]{3,2,1,0:T(8,128)S(1)} %bitcast_subtract_fusion.2), kind=kLoop, calls=%fused_computation.16.clone.1 | loop fusion | flops 524288 | bytes 8388608 | tf_op jit(solution)/shard_map/while/body/neg | solution.py:46
  127.9 11.9 %bitcast_select_fusion.2 = f32[2,64,64,128]{3,2,1,0:T(8,128)} fusion(f32[2,64,64,128]{3,2,1,0:T(8,128)S(1)} %copy.51, f32[2,64,64,64]{3,2,1,0:T(8,128)} %get-tuple-element.147, f32[2,64,64,64]{3,2,1,0:T(8,128)S(1)} %get-tuple-element.148, f32[2,64,64,128]{3,2,1,0:T(8,128)S(1)} %bitcast_subtract_fusion.2, pred[2]{0:T(512)(128)(4,1)S(1)} %broadcast_compare_fusion.2), kind=kOutput, calls=%fused_computation.17.clone.1 | convolution fusion | flops 1615855616 | bytes 16777218 | tf_op jit(solution)/shard_map/while/body/...ij,...jl->...il/dot_general | solution.py:51
  140.4 2.2 copy.51
  142.6 1.4 slice_negate_fusion.4
  144.0 9.0 %bitcast_subtract_fusion.2 = f32[2,64,64,128]{3,2,1,0:T(8,128)S(1)} fusion(f32[64,128]{1,0:T(8,128)S(1)} %get-tuple-element.171, f32[2,64,128]{2,1,0:T(8,128)S(1)} %get-tuple-element.174, f32[64,64,128]{2,1,0:T(8,128)S(1)} %get-tuple-element.172, f32[2,64,128]{2,1,0:T(8,128)S(1)} %get-tuple-element.173, ...), kind=kOutput, calls=%fused_computation.18.clone.1 | convolution fusion | flops 1617952768 | bytes 14843904 | tf_op jit(solution)/shard_map/while/body/...ij,...jl->...il/dot_general | solution.py:51
  153.0 3.5 %slice_negate_fusion.5 = (f32[2,64,64,64]{3,2,1,0:T(8,128)S(1)}, f32[2,64,64,64]{3,2,1,0:T(8,128)}) fusion(f32[2,64,64,128]{3,2,1,0:T(8,128)S(1)} %bitcast_subtract_fusion.2), kind=kLoop, calls=%fused_computation.16.clone.1 | loop fusion | flops 524288 | bytes 8388608 | tf_op jit(solution)/shard_map/while/body/neg | solution.py:46
  156.5 11.9 %bitcast_select_fusion.2 = f32[2,64,64,128]{3,2,1,0:T(8,128)} fusion(f32[2,64,64,128]{3,2,1,0:T(8,128)S(1)} %copy.51, f32[2,64,64,64]{3,2,1,0:T(8,128)} %get-tuple-element.147, f32[2,64,64,64]{3,2,1,0:T(8,128)S(1)} %get-tuple-element.148, f32[2,64,64,128]{3,2,1,0:T(8,128)S(1)} %bitcast_subtract_fusion.2, pred[2]{0:T(512)(128)(4,1)S(1)} %broadcast_compare_fusion.2), kind=kOutput, calls=%fused_computation.17.clone.1 | convolution fusion | flops 1615855616 | bytes 16777218 | tf_op jit(solution)/shard_map/while/body/...ij,...jl->...il/dot_general | solution.py:51
  169.0 2.2 copy.51
  171.2 1.4 slice_negate_fusion.4
  172.7 9.0 %bitcast_subtract_fusion.2 = f32[2,64,64,128]{3,2,1,0:T(8,128)S(1)} fusion(f32[64,128]{1,0:T(8,128)S(1)} %get-tuple-element.171, f32[2,64,128]{2,1,0:T(8,128)S(1)} %get-tuple-element.174, f32[64,64,128]{2,1,0:T(8,128)S(1)} %get-tuple-element.172, f32[2,64,128]{2,1,0:T(8,128)S(1)} %get-tuple-element.173, ...), kind=kOutput, calls=%fused_computation.18.clone.1 | convolution fusion | flops 1617952768 | bytes 14843904 | tf_op jit(solution)/shard_map/while/body/...ij,...jl->...il/dot_general | solution.py:51
  181.7 3.5 %slice_negate_fusion.5 = (f32[2,64,64,64]{3,2,1,0:T(8,128)S(1)}, f32[2,64,64,64]{3,2,1,0:T(8,128)}) fusion(f32[2,64,64,128]{3,2,1,0:T(8,128)S(1)} %bitcast_subtract_fusion.2), kind=kLoop, calls=%fused_computation.16.clone.1 | loop fusion | flops 524288 | bytes 8388608 | tf_op jit(solution)/shard_map/while/body/neg | solution.py:46
  185.2 11.9 %bitcast_select_fusion.2 = f32[2,64,64,128]{3,2,1,0:T(8,128)} fusion(f32[2,64,64,128]{3,2,1,0:T(8,128)S(1)} %copy.51, f32[2,64,64,64]{3,2,1,0:T(8,128)} %get-tuple-element.147, f32[2,64,64,64]{3,2,1,0:T(8,128)S(1)} %get-tuple-element.148, f32[2,64,64,128]{3,2,1,0:T(8,128)S(1)} %bitcast_subtract_fusion.2, pred[2]{0:T(512)(128)(4,1)S(1)} %broadcast_compare_fusion.2), kind=kOutput, calls=%fused_computation.17.clone.1 | convolution fusion | flops 1615855616 | bytes 16777218 | tf_op jit(solution)/shard_map/while/body/...ij,...jl->...il/dot_general | solution.py:51
  197.9 9.2 %dot_general.18 = f32[2,64,2,64,64]{3,2,1,4,0:T(2,128)} reshape(f32[2,64,128,64]{2,1,3,0:T(8,128)} %bitcast.73) | data formatting | bytes 8388608 | tf_op jit(solution)/shard_map/k,fkij->fij/dot_general | solution.py:118
  207.0 12.3 %fusion.27 = f32[1,2,64,2,64]{4,0,3,2,1:T(1,128)S(1)} fusion(f32[2,64,2,64,64]{3,2,1,4,0:T(2,128)} %dot_general.18, s32[64]{0:T(128)S(1)} %gather_fusion, s32[]{:T(128)S(6)} %axis_index.22), kind=kOutput, calls=%fused_computation.28 | convolution fusion | flops 12583552 | bytes 4260100 | tf_op jit(solution)/shard_map/k,fkij->fij/dot_general | solution.py:118
  219.3 0.1 copy.36
  219.4 0.1 reshape.98
  219.6 8.5 %all_to_all.22 = f32[4,1,4096]{2,1,0:T(1,128)S(1)} all-to-all(f32[4,1,4096]{2,1,0:T(1,128)S(1)} %reshape.98), channel_id=1, replica_groups=mesh['freq'=64,'kgrp'=4] {'kgrp'}, dimensions={0} | all-to-all | bytes 131072 | tf_op jit(solution)/shard_map/all_to_all | solution.py:37
  228.0 0.5 broadcast.217
  228.5 0.8 reduce.1
  229.3 0.1 reshape.99
  229.5 0.8 copy.31
  230.2 5.9 %all-to-all-start.2 = ((f32[2,2,64,1,16]{4,0,1,3,2:T(2,128)}), f32[2,2,64,1,16]{4,0,1,3,2:T(2,128)S(1)}, u32[]{:S(2)}, u32[]{:S(2)}) async-start(f32[2,2,64,1,16]{4,0,1,3,2:T(2,128)} %copy.31), calls=%async_computation.2 | async-start | bytes 262144 | tf_op jit(solution)/shard_map/all_to_all | solution.py:124
  236.1 0.6 convert_reduce_fusion
  236.7 9.8 %all-to-all-done.2 = f32[2,2,64,1,16]{4,0,1,3,2:T(2,128)S(1)} async-done(((f32[2,2,64,1,16]{4,0,1,3,2:T(2,128)}), f32[2,2,64,1,16]{4,0,1,3,2:T(2,128)S(1)}, u32[]{:S(2)}, u32[]{:S(2)}) %all-to-all-start.2) | async-done | bytes 16416 | tf_op jit(solution)/shard_map/all_to_all | solution.py:124
  246.6 0.7 divide_bitcast_fusion
  247.3 0.7 copy.33
  (16 shorter events, 0.2 us)
Async XLA Ops:
  2.3 16.0 %copy-start.1 = (f32[2,64,128]{2,1,0:T(8,128)S(1)}, f32[2,64,128]{2,1,0:T(8,128)}, u32[]{:S(2)}) copy-start(f32[2,64,128]{2,1,0:T(8,128)} %param.8) | copy-start | bytes 196612
  2.3 64.3 %all-to-all-start = ((f32[64,1,64,128]{3,2,1,0:T(8,128)}), f32[64,1,64,128]{3,2,1,0:T(8,128)S(1)}, u32[]{:S(2)}, u32[]{:S(2)}) async-start(f32[64,1,64,128]{3,2,1,0:T(8,128)} %broadcast_in_dim.46), calls=%async_computation | async-start | bytes 4194304 | tf_op jit(solution)/shard_map/all_to_all | solution.py:13
  15.7 5.3 %copy-start = (s32[256]{0:T(256)S(1)}, s32[256]{0:T(256)}, u32[]{:S(2)}) copy-start(s32[256]{0:T(256)} %param.10) | copy-start | bytes 3076
  15.7 6.1 %copy-start.3 = (s32[128]{0:T(128)S(1)}, s32[128]{0:T(128)}, u32[]{:S(2)}) copy-start(s32[128]{0:T(128)} %param.11) | copy-start | bytes 1540
  15.7 6.8 %copy-start.2 = (f32[2,64,128]{2,1,0:T(8,128)S(1)}, f32[2,64,128]{2,1,0:T(8,128)}, u32[]{:S(2)}) copy-start(f32[2,64,128]{2,1,0:T(8,128)} %param.9) | copy-start | bytes 196612
  230.2 16.3 %all-to-all-start.2 = ((f32[2,2,64,1,16]{4,0,1,3,2:T(2,128)}), f32[2,2,64,1,16]{4,0,1,3,2:T(2,128)S(1)}, u32[]{:S(2)}, u32[]{:S(2)}) async-start(f32[2,2,64,1,16]{4,0,1,3,2:T(2,128)} %copy.31), calls=%async_computation.2 | async-start | bytes 262144 | tf_op jit(solution)/shard_map/all_to_all | solution.py:124
where the time goes:
time: 249 us; the launch traced here: 248 us
  matrix products  75 us (30%)
  waiting for transfers between devices  54 us (22%)
  other arithmetic  45.6 us (18%)
  local copies, waits for them, and re-layouts  43.1 us (17%)
  starting transfers between devices  19 us (8%)
  blocking collectives  8.46 us (3%)
  loops' own time  2.77 us (1%)
    dot_general x6, matrix products, complex_product(): jnp.einsum('...ij,...jl->...il', left_side, blockify(right_side), precisi...  62.7 us
    all_to_all x1, waiting for transfers between devices, copy_for_each(): lax.all_to_all(jnp.broadcast_to(value[None], (size, *value.shape)), axis,...  44.1 us
    sub x1, other arithmetic, build_matrix(): return diagonal_shift[:, None] - kpoint_rows[None] - sigma_rows[:, None]  22.3 us
    neg x6, other arithmetic, blockify(): lower_row = jnp.concatenate([-imag_part, real_part], -1)  14.8 us
    all_to_all x1, starting transfers between devices, copy_for_each(): lax.all_to_all(jnp.broadcast_to(value[None], (size, *value.shape)), axis,...  13.1 us
    dot_general x1, matrix products, per_device(): jnp.einsum('k,fkij->fij', factors, inverses, precision=lax.Precision.HIGH...  12.3 us
    all_to_all x1, waiting for transfers between devices, per_device(): lax.all_to_all(quarter, 'freq', split_axis=2, concat_axis=0, tiled=True)  9.85 us
    dot_general x2, local copies, waits for them, and re-layouts, per_device(): jnp.einsum('k,fkij->fij', factors, inverses, precision=lax.Precision.HIGH...  9.26 us
  transfers between devices with their start and end apart: 2, of which 2 were waited for; matrix products, arithmetic and copies ran while one was open for 3% of the time, Pallas kernels for 0%

commit v1 on v0

v1 whole, which is shorter than its diff:
```python
import functools
import math

import jax
import jax.numpy as jnp
from jax import lax
from jax.experimental import pallas as pl
from jax.experimental.pallas import tpu as pltpu
from jax.sharding import PartitionSpec as P

chem_potential = 0.2

NORB = 64
WIDE = 2 * NORB
XS, YS, ZS, CORES = 4, 4, 8, 2
LINE = ZS * CORES
PER_FREQ = 2
N_LOCAL = XS * PER_FREQ
PAIRS = LINE // 2
FREQ = 128
KPTS = 256
BF = jnp.bfloat16
F32 = jnp.float32


def vmem():
    return pl.BlockSpec(memory_space=pltpu.VMEM)


def smem():
    return pl.BlockSpec(memory_space=pltpu.SMEM)


def on_freq(index):
    return {"freq": index}


def greet(targets):
    barrier = pltpu.get_barrier_semaphore()
    for target in targets:
        pl.semaphore_signal(barrier, inc=1, device_id=target, device_id_type=pl.DeviceIdType.MESH)
    pl.semaphore_wait(barrier, len(targets))


def send(src, dst, send_sem, recv_sem, target):
    return pltpu.make_async_remote_copy(
        src_ref=src,
        dst_ref=dst,
        send_sem=send_sem,
        recv_sem=recv_sem,
        device_id=target,
        device_id_type=pl.DeviceIdType.MESH,
    )


Z_ORDER = (4, 3, 5, 2, 6, 1, 7)


def gather_kernel(h_ref, s_ref, g_ref, hall, sall, gall, zs, zr, ps, pr, ss, sr, gs, gr):
    f = lax.axis_index("freq")
    x, t = f // LINE, f % LINE
    z, c = t // CORES, t % CORES
    partner = on_freq(x * LINE + z * CORES + (1 - c))

    def along_z(dz):
        return on_freq(x * LINE + (z + dz) % ZS * CORES + c)

    def along_x(dx):
        return on_freq((x + dx) % XS * LINE + t)

    greet([partner] + [along_z(dz) for dz in range(1, ZS)] + [along_x(dx) for dx in range(1, XS)])
    started = []
    for dz in Z_ORDER:
        copy = send(h_ref.at[0], hall.at[t], zs.at[dz], zr.at[dz], along_z(dz))
        copy.start()
        started.append(copy)
    copy = send(h_ref.at[0], hall.at[t], ps.at[0], pr.at[0], partner)
    copy.start()
    started.append(copy)
    mine = pl.ds(x * PER_FREQ, PER_FREQ)
    for dx in (2, 1, 3):
        for src, dst, s_sem, r_sem in ((g_ref, gall, gs, gr), (s_ref, sall, ss, sr)):
            copy = send(src, dst.at[mine], s_sem.at[dx], r_sem.at[dx], along_x(dx))
            copy.start()
            started.append(copy)
    hall[pl.ds(t, 1)] = h_ref[...]
    sall[mine] = s_ref[...]
    gall[mine] = g_ref[...]
    for dz in (1, 7, 2, 6, 3, 5, 4):
        source = (z + ZS - dz) % ZS * CORES + c
        send(h_ref.at[0], hall.at[source], zs.at[dz], zr.at[dz], along_z(dz)).wait_recv()
        copy = send(hall.at[source], hall.at[source], ps.at[dz], pr.at[dz], partner)
        copy.start()
        started.append(copy)
    for dx in (1, 3, 2):
        theirs = pl.ds((x + XS - dx) % XS * PER_FREQ, PER_FREQ)
        for src, dst, s_sem, r_sem in ((g_ref, gall, gs, gr), (s_ref, sall, ss, sr)):
            send(src, dst.at[theirs], s_sem.at[dx], r_sem.at[dx], along_x(dx)).wait_recv()
    for dz in range(ZS):
        source = (z + ZS - dz) % ZS * CORES + (1 - c)
        send(h_ref.at[0], hall.at[source], ps.at[dz], pr.at[dz], partner).wait_recv()
    for copy in started:
        copy.wait_send()


def gather(hamiltonian, self_energy, guess_factor):
    dma = pltpu.SemaphoreType.DMA
    return pl.pallas_call(
        gather_kernel,
        name="gather",
        out_shape=(
            jax.ShapeDtypeStruct((LINE, NORB, WIDE), F32),
            jax.ShapeDtypeStruct((N_LOCAL, NORB, WIDE), F32),
            jax.ShapeDtypeStruct((N_LOCAL, NORB, WIDE), F32),
        ),
        in_specs=[vmem()] * 3,
        out_specs=(vmem(),) * 3,
        scratch_shapes=[dma((ZS,))] * 4 + [dma((XS,))] * 4,
        compiler_params=pltpu.CompilerParams(collective_id=0, has_side_effects=True),
    )(hamiltonian, self_energy, guess_factor)


def halves(value):
    high = value.astype(BF)
    low = (value - high.astype(F32)).astype(BF)
    return high, low


def dot(left, right):
    return jnp.dot(left, right, preferred_element_type=F32)


def product3(left, right):
    left_high, left_low = left
    right_high, right_low = right
    return dot(
        jnp.concatenate([left_high, left_low], 1), jnp.concatenate([right_high, right_high], 0)
    ) + dot(left_high, right_low)


def invert_kernel(w_ref, n_ref, h_ref, s_ref, g_ref, out_ref, wh, wl, hcol, hrow, gcat, gz, zcol, zrow, er_ref, ei_ref, gh_ref, x_ref):
    f = lax.axis_index("freq")
    y = lax.axis_index("kgrp")
    x, t = f // LINE, f % LINE
    rows = lax.broadcasted_iota(jnp.int32, (NORB, WIDE), 0)
    lanes = lax.broadcasted_iota(jnp.int32, (NORB, WIDE), 1)
    first = lanes < NORB
    eye_mask = rows == lanes % NORB
    eye = eye_mask.astype(F32)
    first_bf = first.astype(F32).astype(BF)
    second_bf = (1.0 - first.astype(F32)).astype(BF)

    def swap(value):
        return pltpu.roll(value, NORB, 1)

    def paired(one, two):
        return jnp.where(first, one, swap(two)), jnp.where(first, swap(one), two)

    def as_right(real, imag):
        real_high, real_low = halves(real)
        imag_high, imag_low = halves(imag)
        high = jnp.concatenate(
            [jnp.concatenate([real_high, imag_high], 1), jnp.concatenate([-imag_high, real_high], 1)], 0
        )
        low = jnp.concatenate(
            [jnp.concatenate([real_low, imag_low], 1), jnp.concatenate([-imag_low, real_low], 1)], 0
        )
        return high, low

    def diagonal_columns(value):
        kept = jnp.where(eye_mask, value, 0.0)
        left = jnp.sum(jnp.where(first, kept, 0.0), 1, keepdims=True)
        right = jnp.sum(jnp.where(first, 0.0, kept), 1, keepdims=True)
        return jnp.where(first, left, right)

    def diagonal_row(value):
        return jnp.sum(jnp.where(eye_mask, value, 0.0), 0, keepdims=True)

    def add_up(i, total):
        for j in range(16):
            total = total + w_ref[i * 16 + j]
        return total

    inv_total = 1.0 / lax.fori_loop(0, KPTS // 16, add_up, jnp.int32(0)).astype(F32)

    def prepare_pair(p, carry):
        real, imag = paired(h_ref[2 * p], h_ref[2 * p + 1])
        high, low = as_right(real, imag)
        wh[p] = high
        wl[p] = low
        hcol[p] = diagonal_columns(real)
        hrow[p] = jnp.broadcast_to(diagonal_row(real), (8, WIDE))
        return carry

    lax.fori_loop(0, PAIRS, prepare_pair, 0)

    def prepare_freq(n, carry):
        freq_id = n // PER_FREQ * (PER_FREQ * LINE) + t * PER_FREQ + n % PER_FREQ
        matsubara = (2 * freq_id + 1).astype(F32) * (math.pi / (2 * FREQ))
        shift = jnp.where(first, chem_potential, matsubara)
        zed = jnp.where(eye_mask, shift, 0.0) - s_ref[n]
        real, imag = paired(zed, zed)
        g_high, g_low = halves(g_ref[n])
        gz[n] = product3((g_high, g_low), as_right(real, imag))
        gcat[n] = jnp.concatenate([g_high, g_low], 1)
        zcol[n] = jnp.concatenate([diagonal_columns(real), diagonal_columns(imag)], 1)
        row = jnp.concatenate([diagonal_row(real), diagonal_row(imag)], 1)
        zrow[n] = jnp.broadcast_to(row, (8, 2 * WIDE))
        return carry

    lax.fori_loop(0, N_LOCAL, prepare_freq, 0)

    def residual_pair(p, carry):
        left = gcat[...].reshape(N_LOCAL * NORB, 2 * WIDE)
        high = wh[p]
        gh_ref[...] = dot(left, jnp.concatenate([high, high], 0)) + dot(left[:, :WIDE], wl[p])
        h_diag = hcol[p]

        def one_freq(n, inner):
            gh = gh_ref[pl.ds(pl.multiple_of(n * NORB, NORB), NORB)]
            a = gz[n] - gh
            a_real, a_imag = a[:, :WIDE], a[:, WIDE:]
            d = zcol[n]
            d_real, d_imag = d[:, :WIDE] - h_diag, d[:, WIDE:]
            inv = 1.0 / (d_real * d_real + d_imag * d_imag)
            v_real, v_imag = d_real * inv, d_imag * inv
            er_ref[n, p] = eye - (v_real * a_real + v_imag * a_imag)
            ei_ref[n, p] = v_imag * a_real - v_real * a_imag
            return inner

        return lax.fori_loop(0, N_LOCAL, one_freq, carry, unroll=2)

    lax.fori_loop(0, PAIRS, residual_pair, 0)

    def column_scale(n, p):
        d = zrow[n]
        d_real, d_imag = d[:, :WIDE] - hrow[p], d[:, WIDE:]
        kpt = (x * LINE + 2 * p) * YS + y
        w_one = w_ref[kpt].astype(F32) * inv_total
        w_two = w_ref[kpt + YS].astype(F32) * inv_total
        weight = jnp.where(first[:8], w_one, w_two)
        inv = weight / (d_real * d_real + d_imag * d_imag)
        return (d_real * inv)[:1], (-d_imag * inv)[:1]

    def right_blocks(real, imag):
        def build(r, i):
            return jnp.concatenate(
                [
                    jnp.concatenate([r * first_bf, i * first_bf], 1),
                    jnp.concatenate([r * second_bf, i * second_bf], 1),
                ],
                0,
            )

        r_high, r_low = halves(real)
        i_high, i_low = halves(imag)
        return build(r_high, i_high), build(r_low, i_low)

    def left_rows(real, imag):
        return halves(jnp.concatenate([real, imag], 0))

    def combine(out):
        return out[:NORB, :WIDE] - out[NORB:, WIDE:], out[:NORB, WIDE:] + out[NORB:, :WIDE]

    def series(steps, e_real, e_imag):
        q_real, q_imag = eye + e_real, e_imag
        if steps == 1:
            return q_real, q_imag
        p_real, p_imag = combine(product3(left_rows(e_real, e_imag), right_blocks(e_real, e_imag)))
        for level in range(steps - 1):
            right = right_blocks(p_real, p_imag)
            t_real, t_imag = combine(product3(left_rows(q_real, q_imag), right))
            if level < steps - 2:
                p_real, p_imag = combine(product3(left_rows(p_real, p_imag), right))
            q_real, q_imag = q_real + t_real, q_imag + t_imag
        return q_real, q_imag

    def one_freq_sum(n, carry):
        freq_id = n // PER_FREQ * (PER_FREQ * LINE) + t * PER_FREQ + n % PER_FREQ
        count = n_ref[freq_id]

        def summed(steps):
            def body(p, total):
                t_real, t_imag = total
                q_real, q_imag = series(steps, er_ref[n, p], ei_ref[n, p])
                u_real, u_imag = column_scale(n, p)
                return (
                    t_real + (q_real * u_real - q_imag * u_imag),
                    t_imag + (q_real * u_imag + q_imag * u_real),
                )

            zero = jnp.zeros((NORB, WIDE), F32)
            t_real, t_imag = lax.fori_loop(0, PAIRS, body, (zero, zero), unroll=2)
            g = g_ref[n]
            turned = jnp.where(first, -swap(g), swap(g))
            right = jnp.concatenate([g, g, turned, turned], 0)
            r_high, r_low = halves(right)
            l_high, l_low = halves(jnp.concatenate([t_real, t_imag], 1))
            x_ref[n] = dot(l_high, r_high) + dot(l_low, r_high) + dot(l_high, r_low)

        for steps in (1, 2, 3):
            pl.when(count == steps)(functools.partial(summed, steps))
        return carry

    lax.fori_loop(0, N_LOCAL, one_freq_sum, 0)

    quarter = lanes % NORB // (NORB // YS)
    for n_high in range(2):
        for to_y in range(YS):
            mixed = None
            for n_low in range(4):
                value = x_ref[n_high * 4 + n_low]
                shift = (n_low - to_y) * (NORB // YS) % WIDE
                moved = pltpu.roll(value, shift, 1) if shift else value
                mixed = moved if mixed is None else jnp.where(quarter == n_low, moved, mixed)
            for to_x in range(XS):
                out_ref[to_x, to_y, n_high] = mixed[to_x * LINE : (to_x + 1) * LINE]


def invert(weights, counts, h_all, s_all, g_all):
    return pl.pallas_call(
        invert_kernel,
        name="invert",
        out_shape=jax.ShapeDtypeStruct((XS, YS, 2, LINE, WIDE), F32),
        in_specs=[smem(), smem(), vmem(), vmem(), vmem()],
        out_specs=vmem(),
        scratch_shapes=[
            pltpu.VMEM((PAIRS, WIDE, 2 * WIDE), BF),
            pltpu.VMEM((PAIRS, WIDE, 2 * WIDE), BF),
            pltpu.VMEM((PAIRS, NORB, WIDE), F32),
            pltpu.VMEM((PAIRS, 8, WIDE), F32),
            pltpu.VMEM((N_LOCAL, NORB, 2 * WIDE), BF),
            pltpu.VMEM((N_LOCAL, NORB, 2 * WIDE), F32),
            pltpu.VMEM((N_LOCAL, NORB, 2 * WIDE), F32),
            pltpu.VMEM((N_LOCAL, 8, 2 * WIDE), F32),
            pltpu.VMEM((N_LOCAL, PAIRS, NORB, WIDE), F32),
            pltpu.VMEM((N_LOCAL, PAIRS, NORB, WIDE), F32),
            pltpu.VMEM((N_LOCAL * NORB, 2 * WIDE), F32),
            pltpu.VMEM((N_LOCAL, NORB, WIDE), F32),
        ],
    )(weights, counts, h_all, s_all, g_all)


def exit_kernel(o_ref, q_ref, landed, rows_ref, as_, ar, bs, br):
    f = lax.axis_index("freq")
    y = lax.axis_index("kgrp")
    x, t = f // LINE, f % LINE
    z, c = t // CORES, t % CORES
    plane = [(dx, dy) for dx in range(XS) for dy in range(YS) if dx or dy]
    line = [(dz, dc) for dz in range(ZS) for dc in range(CORES) if dz or dc]

    def in_plane(dx, dy):
        return {"freq": (x + dx) % XS * LINE + t, "kgrp": (y + dy) % YS}

    def place(dz, dc):
        return (z + dz) % ZS * CORES + (c + dc) % CORES

    greet([in_plane(*d) for d in plane] + [on_freq(x * LINE + place(*d)) for d in line])
    started = []
    for dx, dy in plane:
        slot = dx * YS + dy
        copy = send(
            o_ref.at[(x + dx) % XS, (y + dy) % YS], landed.at[slot], as_.at[slot], ar.at[slot], in_plane(dx, dy)
        )
        copy.start()
        started.append(copy)
    total = o_ref[x, y]
    for dx, dy in plane:
        slot = dx * YS + dy
        send(o_ref.at[x, y], landed.at[slot], as_.at[slot], ar.at[slot], in_plane(dx, dy)).wait_recv()
        total = total + landed[slot]
    for to in range(LINE):
        for n_high in range(2):
            rows_ref[to, n_high : n_high + 1] = total[n_high, to : to + 1]
    for dz, dc in line:
        slot = dz * CORES + dc
        to = place(dz, dc)
        copy = send(rows_ref.at[to], q_ref.at[t], bs.at[slot], br.at[slot], on_freq(x * LINE + to))
        copy.start()
        started.append(copy)
    q_ref[pl.ds(t, 1)] = rows_ref[pl.ds(t, 1)]
    for dz, dc in line:
        slot = dz * CORES + dc
        source = (z + ZS - dz) % ZS * CORES + (c + CORES - dc) % CORES
        send(rows_ref.at[source], q_ref.at[source], bs.at[slot], br.at[slot], on_freq(x * LINE + place(dz, dc))).wait_recv()
    for copy in started:
        copy.wait_send()


def leave(sums):
    dma = pltpu.SemaphoreType.DMA
    return pl.pallas_call(
        exit_kernel,
        name="leave",
        out_shape=jax.ShapeDtypeStruct((LINE, 2, WIDE), F32),
        in_specs=[vmem()],
        out_specs=vmem(),
        scratch_shapes=[
            pltpu.VMEM((XS * YS, 2, LINE, WIDE), F32),
            pltpu.VMEM((LINE, 2, WIDE), F32),
            dma((XS * YS,)),
            dma((XS * YS,)),
            dma((LINE,)),
            dma((LINE,)),
        ],
        compiler_params=pltpu.CompilerParams(collective_id=1, has_side_effects=True),
    )(sums)


def per_device(hamiltonian, self_energy, guess_factor, weights, counts):
    h_all, s_all, g_all = gather(hamiltonian, self_energy, guess_factor)
    sums = invert(weights, counts, h_all, s_all, g_all)
    arrived = leave(sums)
    pieces = arrived.reshape(LINE, 2, 2, 2, 2, NORB // YS)
    return pieces.transpose(5, 2, 1, 3, 0, 4).reshape(NORB // YS, 2 * FREQ)


def solution(mesh):
    return jax.shard_map(
        per_device,
        mesh=mesh,
        in_specs=(
            P(("freq", "kgrp"), None, None),
            P("freq", None, None),
            P("freq", None, None),
            P(),
            P(),
        ),
        out_specs=P(("freq", "kgrp"), None),
        check_vma=False,
    )
```

time: 249 us -> 65.5 us (0.26)
  matrix products: 75 us -> 0 us
  Pallas kernels: 0 us -> 62.5 us
  waiting for transfers between devices: 54 us -> 0 us
  other arithmetic: 45.6 us -> 0 us
  local copies, waits for them, and re-layouts: 43.1 us -> 1.66 us
  starting transfers between devices: 19 us -> 0 us
  blocking collectives: 8.46 us -> 0 us
  loops' own time: 2.77 us -> 0 us
    dot_general x7 -> x0, matrix products: 75 us -> none  [the longest x6 62.7 us: complex_product(): jnp.einsum('...ij,...jl->...il', left_side, blockify(right_side), precisi...]
    pallas_call x0 -> x3, Pallas kernels: none -> 62.5 us  [the longest x1 23.3 us: leave(): pl.pallas_call(exit_kernel, name='leave', out_shape=jax.ShapeDtypeStruct(...]
    all_to_all x2 -> x0, waiting for transfers between devices: 54 us -> none  [the longest x1 44.1 us: copy_for_each(): lax.all_to_all(jnp.broadcast_to(value[None], (size, *value.shape)), axis,...]
    sub x2 -> x0, other arithmetic: 24.7 us -> none  [the longest x1 22.3 us: build_matrix(): return diagonal_shift[:, None] - kpoint_rows[None] - sigma_rows[:, None]]
    all_to_all x2 -> x0, starting transfers between devices: 19 us -> none  [the longest x1 13.1 us: copy_for_each(): lax.all_to_all(jnp.broadcast_to(value[None], (size, *value.shape)), axis,...]
    neg x6 -> x0, other arithmetic: 14.8 us -> none  [blockify(): lower_row = jnp.concatenate([-imag_part, real_part], -1)]
    dot_general x2 -> x0, local copies, waits for them, and re-layouts: 9.26 us -> none  [per_device(): jnp.einsum('k,fkij->fij', factors, inverses, precision=lax.Precision.HIGH...]
    all_to_all x1 -> x0, blocking collectives: 8.46 us -> none  [summed_on_arrival(): lax.all_to_all(pieces, axis, split_axis=0, concat_axis=0, tiled=True)]
  transfers between devices with their start and end apart: 2 -> 0, of which waited for: 2 -> 0; matrix products, arithmetic and copies ran while one was open for 3% -> 0% of each run, Pallas kernels for 0% -> 0%
where the time goes in v1:
time: 65.5 us; the launch traced here: 64.2 us
  Pallas kernels  62.5 us (95%)
  local copies, waits for them, and re-layouts  1.66 us (3%)
    pallas_call x1, Pallas kernels, leave(): pl.pallas_call(exit_kernel, name='leave', out_shape=jax.ShapeDtypeStruct(...  23.3 us
    pallas_call x1, Pallas kernels, gather(): pl.pallas_call(gather_kernel, name='gather', out_shape=(jax.ShapeDtypeStr...  19.7 us
    pallas_call x1, Pallas kernels, invert(): pl.pallas_call(invert_kernel, name='invert', out_shape=jax.ShapeDtypeStru...  19.5 us

profile of v1, /device:TPU:1, one launch (start us, length us, event | category | flops | bytes accessed | tf_op | source)
XLA Modules:
  0.0 64.2 jit_solution(11389398233927533562)
XLA Ops:
  0.0 19.7 %gather.1 = (f32[16,64,128]{2,1,0:T(8,128)}, f32[8,64,128]{2,1,0:T(8,128)}, f32[8,64,128]{2,1,0:T(8,128)}) custom-call(f32[1,64,128]{2,1,0:T(8,128)} %h_ref.1, f32[2,64,128]{2,1,0:T(8,128)} %s_ref.1, f32[2,64,128]{2,1,0:T(8,128)} %g_ref.1), custom_call_target="tpu_custom_call" | custom-call | tf_op jit(solution)/shard_map/gather/pallas_call | solution.py:108
  19.7 19.5 %invert.1.o_ref = f32[4,4,2,16,128]{4,3,2,1,0:T(8,128)} custom-call(s32[256]{0:T(256)} %w_ref.1, s32[128]{0:T(128)} %n_ref.1, f32[16,64,128]{2,1,0:T(8,128)} %get-tuple-element.8.h_ref, f32[8,64,128]{2,1,0:T(8,128)} %get-tuple-element.9.s_ref, f32[8,64,128]{2,1,0:T(8,128)} %get-tuple-element.10.g_ref), custom_call_target="tpu_custom_call" | custom-call | tf_op jit(solution)/shard_map/invert/pallas_call | solution.py:321
  39.2 23.3 %leave.1 = f32[16,2,128]{2,1,0:T(2,128)} custom-call(f32[4,4,2,16,128]{4,3,2,1,0:T(8,128)} %invert.1.o_ref), custom_call_target="tpu_custom_call" | custom-call | tf_op jit(solution)/shard_map/leave/pallas_call | solution.py:392
  62.6 0.9 %reshape.6 = f32[16,2,2,2,2,16]{5,4,3,2,1,0:T(2,128)S(1)} reshape(f32[16,2,128]{2,1,0:T(2,128)} %leave.1) | data formatting | bytes 32768 | tf_op jit(solution)/shard_map/reshape | solution.py:414
  63.5 0.7 %copy.8 = f32[16,256]{1,0:T(8,128)} copy(f32[16,256]{0,1:T(8,128)S(1)} %bitcast.3) | data formatting | bytes 32768 | tf_op jit(solution)/shard_map/reshape | solution.py:415
  (1 shorter events, 0.0 us)

commit v2 on v1

v2 whole, which is shorter than its diff:
```python
import functools
import math

import jax
import jax.numpy as jnp
from jax import lax
from jax.experimental import pallas as pl
from jax.experimental.pallas import tpu as pltpu
from jax.sharding import PartitionSpec as P

chem_potential = 0.2

NORB = 64
WIDE = 2 * NORB
XS, YS, ZS, CORES = 4, 4, 8, 2
LINE = ZS * CORES
PER_FREQ = 2
N_LOCAL = XS * PER_FREQ
PAIRS = LINE // 2
FREQ = 128
KPTS = 256
BF = jnp.bfloat16
F32 = jnp.float32


def vmem():
    return pl.BlockSpec(memory_space=pltpu.VMEM)


def smem():
    return pl.BlockSpec(memory_space=pltpu.SMEM)


def on_freq(index):
    return {"freq": index}


def greet(targets):
    barrier = pltpu.get_barrier_semaphore()
    for target in targets:
        pl.semaphore_signal(barrier, inc=1, device_id=target, device_id_type=pl.DeviceIdType.MESH)
    pl.semaphore_wait(barrier, len(targets))


def send(src, dst, send_sem, recv_sem, target):
    return pltpu.make_async_remote_copy(
        src_ref=src,
        dst_ref=dst,
        send_sem=send_sem,
        recv_sem=recv_sem,
        device_id=target,
        device_id_type=pl.DeviceIdType.MESH,
    )


Z_ORDER = (4, 3, 5, 2, 6, 1, 7)


def halves(value):
    high = value.astype(BF)
    low = (value - high.astype(F32)).astype(BF)
    return high, low


def dot(left, right):
    return jnp.dot(left, right, preferred_element_type=F32)


def product3(left, right):
    left_high, left_low = left
    right_high, right_low = right
    return dot(
        jnp.concatenate([left_high, left_low], 1), jnp.concatenate([right_high, right_high], 0)
    ) + dot(left_high, right_low)


def swap(value):
    return pltpu.roll(value, NORB, 1)


def lane_masks():
    rows = lax.broadcasted_iota(jnp.int32, (NORB, WIDE), 0)
    lanes = lax.broadcasted_iota(jnp.int32, (NORB, WIDE), 1)
    return lanes, lanes < NORB, rows == lanes % NORB


def gather_kernel(
    w_ref, h_ref, s_ref, g_ref,
    gall, er_ref, ei_ref, ur_ref, ui_ref, tr_ref, ti_ref,
    hall, sall, wh, wl, hcol, hrow, gcat, gz, zcol, zrow, gh_ref,
    zs, zr, ps, pr, ss, sr, gs, gr,
):
    f = lax.axis_index("freq")
    y = lax.axis_index("kgrp")
    x, t = f // LINE, f % LINE
    z, c = t // CORES, t % CORES
    partner = on_freq(x * LINE + z * CORES + (1 - c))
    _, first, eye_mask = lane_masks()
    eye = eye_mask.astype(F32)

    def along_z(dz):
        return on_freq(x * LINE + (z + dz) % ZS * CORES + c)

    def along_x(dx):
        return on_freq((x + dx) % XS * LINE + t)

    def paired(one, two):
        return jnp.where(first, one, swap(two)), jnp.where(first, swap(one), two)

    def as_right(real, imag):
        def build(r, i):
            return jnp.concatenate([jnp.concatenate([r, i], 1), jnp.concatenate([-i, r], 1)], 0)

        real_high, real_low = halves(real)
        imag_high, imag_low = halves(imag)
        return build(real_high, imag_high), build(real_low, imag_low)

    def diagonal_columns(value):
        kept = jnp.where(eye_mask, value, 0.0)
        left = jnp.sum(jnp.where(first, kept, 0.0), 1, keepdims=True)
        right = jnp.sum(jnp.where(first, 0.0, kept), 1, keepdims=True)
        return jnp.where(first, left, right)

    def diagonal_row(value):
        return jnp.sum(jnp.where(eye_mask, value, 0.0), 0, keepdims=True)

    def prepare_freqs(dx):
        owner = (x + XS - dx) % XS
        for b in range(PER_FREQ):
            n = dx * PER_FREQ + b
            matsubara = (2 * (owner * (PER_FREQ * LINE) + t * PER_FREQ + b) + 1).astype(F32) * (
                math.pi / (2 * FREQ)
            )
            shift = jnp.where(first, chem_potential, matsubara)
            zed = jnp.where(eye_mask, shift, 0.0) - sall[n]
            real, imag = paired(zed, zed)
            g_high, g_low = halves(gall[n])
            gz[n] = product3((g_high, g_low), as_right(real, imag))
            gcat[n] = jnp.concatenate([g_high, g_low], 1)
            zcol[n] = jnp.concatenate([diagonal_columns(real), diagonal_columns(imag)], 1)
            zrow[n : n + 1] = jnp.concatenate([diagonal_row(real), diagonal_row(imag)], 1)

    def prepare_pair(p):
        real, imag = paired(hall[p, 0], hall[p, 1])
        high, low = as_right(real, imag)
        wh[p] = high
        wl[p] = low
        hcol[p] = diagonal_columns(real)
        hrow[p : p + 1] = diagonal_row(real)

    def signal_all(targets):
        barrier = pltpu.get_barrier_semaphore()
        for target in targets:
            pl.semaphore_signal(barrier, inc=1, device_id=target, device_id_type=pl.DeviceIdType.MESH)
        return barrier

    greeted = [partner] + [along_z(dz) for dz in range(1, ZS)] + [along_x(dx) for dx in range(1, XS)]
    barrier = signal_all(greeted)
    hall[0, 0] = h_ref[0]
    sall[:PER_FREQ] = s_ref[...]
    gall[:PER_FREQ] = g_ref[...]
    prepare_freqs(0)

    def add_up(i, total):
        for j in range(16):
            total = total + w_ref[i * 16 + j]
        return total

    inv_total = 1.0 / lax.fori_loop(0, KPTS // 16, add_up, jnp.int32(0)).astype(F32)
    tr_ref[...] = jnp.zeros_like(tr_ref)
    ti_ref[...] = jnp.zeros_like(ti_ref)
    pl.semaphore_wait(barrier, len(greeted))

    started = []
    for dz in Z_ORDER:
        copy = send(h_ref.at[0], hall.at[dz, 0], zs.at[dz], zr.at[dz], along_z(dz))
        copy.start()
        started.append(copy)
    copy = send(h_ref.at[0], hall.at[0, 1], ps.at[0], pr.at[0], partner)
    copy.start()
    started.append(copy)

    def freq_copies(dx):
        rows = pl.ds(dx * PER_FREQ, PER_FREQ)
        return (
            send(g_ref, gall.at[rows], gs.at[dx], gr.at[dx], along_x(dx)),
            send(s_ref, sall.at[rows], ss.at[dx], sr.at[dx], along_x(dx)),
        )

    for dx in (2, 1, 3):
        for copy in freq_copies(dx):
            copy.start()
            started.append(copy)

    def arrived_z(dz):
        send(h_ref.at[0], hall.at[dz, 0], zs.at[dz], zr.at[dz], along_z(dz)).wait_recv()
        copy = send(hall.at[dz, 0], hall.at[dz, 1], ps.at[dz], pr.at[dz], partner)
        copy.start()
        started.append(copy)

    def arrived_x(dx):
        for copy in freq_copies(dx):
            copy.wait_recv()
        prepare_freqs(dx)

    def arrived_partner(dz):
        send(h_ref.at[0], hall.at[dz, 1], ps.at[dz], pr.at[dz], partner).wait_recv()
        prepare_pair(dz)

    for dz in (1, 7, 2, 6):
        arrived_z(dz)
    arrived_partner(0)
    arrived_x(1)
    for dz in (3, 5):
        arrived_z(dz)
    arrived_x(3)
    arrived_z(4)
    arrived_x(2)
    for dz in (1, 7, 2, 6, 3, 5, 4):
        arrived_partner(dz)

    def residual_pair(p, carry):
        left = gcat[...].reshape(N_LOCAL * NORB, 2 * WIDE)
        high = wh[p]
        gh_ref[...] = dot(left, jnp.concatenate([high, high], 0)) + dot(left[:, :WIDE], wl[p])
        h_diag = hcol[p]
        chip = x * LINE + (z + ZS - p) % ZS * CORES
        w_one = w_ref[(chip + c) * YS + y].astype(F32) * inv_total
        w_two = w_ref[(chip + 1 - c) * YS + y].astype(F32) * inv_total
        weight = jnp.where(first[:N_LOCAL], w_one, w_two)
        d_real, d_imag = zrow[:, :WIDE] - hrow[pl.ds(p, 1)], zrow[:, WIDE:]
        inv = weight / (d_real * d_real + d_imag * d_imag)
        ur_ref[p] = d_real * inv
        ui_ref[p] = -d_imag * inv
        for n in range(N_LOCAL):
            a = gz[n] - gh_ref[n * NORB : (n + 1) * NORB]
            a_real, a_imag = a[:, :WIDE], a[:, WIDE:]
            d = zcol[n]
            d_real, d_imag = d[:, :WIDE] - h_diag, d[:, WIDE:]
            inv = 1.0 / (d_real * d_real + d_imag * d_imag)
            v_real, v_imag = d_real * inv, d_imag * inv
            e_real = eye - (v_real * a_real + v_imag * a_imag)
            e_imag = v_imag * a_real - v_real * a_imag
            er_ref[n, p] = e_real
            ei_ref[n, p] = e_imag
            u_real, u_imag = ur_ref[p, n : n + 1], ui_ref[p, n : n + 1]
            q_real = eye + e_real
            tr_ref[n] += q_real * u_real - e_imag * u_imag
            ti_ref[n] += q_real * u_imag + e_imag * u_real
        return carry

    lax.fori_loop(0, PAIRS, residual_pair, 0)
    for copy in started:
        copy.wait_send()


def gather(weights, hamiltonian, self_energy, guess_factor):
    dma = pltpu.SemaphoreType.DMA
    powers = jax.ShapeDtypeStruct((N_LOCAL, PAIRS, NORB, WIDE), F32)
    scales = jax.ShapeDtypeStruct((PAIRS, N_LOCAL, WIDE), F32)
    totals = jax.ShapeDtypeStruct((N_LOCAL, NORB, WIDE), F32)
    return pl.pallas_call(
        gather_kernel,
        name="gather",
        out_shape=(totals, powers, powers, scales, scales, totals, totals),
        in_specs=[smem()] + [vmem()] * 3,
        out_specs=(vmem(),) * 7,
        scratch_shapes=[
            pltpu.VMEM((ZS, CORES, NORB, WIDE), F32),
            pltpu.VMEM((N_LOCAL, NORB, WIDE), F32),
            pltpu.VMEM((PAIRS, WIDE, 2 * WIDE), BF),
            pltpu.VMEM((PAIRS, WIDE, 2 * WIDE), BF),
            pltpu.VMEM((PAIRS, NORB, WIDE), F32),
            pltpu.VMEM((PAIRS, WIDE), F32),
            pltpu.VMEM((N_LOCAL, NORB, 2 * WIDE), BF),
            pltpu.VMEM((N_LOCAL, NORB, 2 * WIDE), F32),
            pltpu.VMEM((N_LOCAL, NORB, 2 * WIDE), F32),
            pltpu.VMEM((N_LOCAL, 2 * WIDE), F32),
            pltpu.VMEM((N_LOCAL * NORB, 2 * WIDE), F32),
        ]
        + [dma((ZS,))] * 4
        + [dma((XS,))] * 4,
        compiler_params=pltpu.CompilerParams(
            collective_id=0, has_side_effects=True, vmem_limit_bytes=20 << 20
        ),
    )(weights, hamiltonian, self_energy, guess_factor)


def power_kernel(n_ref, g_ref, er_ref, ei_ref, ur_ref, ui_ref, t1r_ref, t1i_ref, out_ref, sr_ref, si_ref, qr_ref, qi_ref, tr_ref, ti_ref):
    f = lax.axis_index("freq")
    x, t = f // LINE, f % LINE
    lanes, first, eye_mask = lane_masks()
    eye = eye_mask.astype(F32)
    first_bf = first.astype(F32).astype(BF)
    second_bf = (1.0 - first.astype(F32)).astype(BF)

    def right_blocks(real, imag):
        def build(r, i):
            return jnp.concatenate(
                [
                    jnp.concatenate([r * first_bf, i * first_bf], 1),
                    jnp.concatenate([r * second_bf, i * second_bf], 1),
                ],
                0,
            )

        r_high, r_low = halves(real)
        i_high, i_low = halves(imag)
        return build(r_high, i_high), build(r_low, i_low)

    def left_rows(real, imag):
        return halves(jnp.concatenate([real, imag], 0))

    def combine(out):
        return out[:NORB, :WIDE] - out[NORB:, WIDE:], out[:NORB, WIDE:] + out[NORB:, :WIDE]

    def weighted(n, p, real, imag):
        u_real, u_imag = ur_ref[p, pl.ds(n, 1)], ui_ref[p, pl.ds(n, 1)]
        return real * u_real - imag * u_imag, real * u_imag + imag * u_real

    def two_steps(n):
        for p in range(PAIRS):
            e_real, e_imag = er_ref[n, p], ei_ref[n, p]
            sr_ref[p], si_ref[p] = combine(product3(left_rows(e_real, e_imag), right_blocks(e_real, e_imag)))
        total = t1r_ref[n], t1i_ref[n]
        for p in range(PAIRS):
            left = left_rows(eye + er_ref[n, p], ei_ref[n, p])
            real, imag = combine(product3(left, right_blocks(sr_ref[p], si_ref[p])))
            real, imag = weighted(n, p, real, imag)
            total = total[0] + real, total[1] + imag
        tr_ref[n], ti_ref[n] = total

    def three_steps(n):
        for p in range(PAIRS):
            e_real, e_imag = er_ref[n, p], ei_ref[n, p]
            sr_ref[p], si_ref[p] = combine(product3(left_rows(e_real, e_imag), right_blocks(e_real, e_imag)))
        for p in range(PAIRS):
            e_real, e_imag = er_ref[n, p], ei_ref[n, p]
            s_real, s_imag = sr_ref[p], si_ref[p]
            right = right_blocks(s_real, s_imag)
            real, imag = combine(product3(left_rows(eye + e_real, e_imag), right))
            qr_ref[p], qi_ref[p] = eye + e_real + real, e_imag + imag
            sr_ref[p], si_ref[p] = combine(product3(left_rows(s_real, s_imag), right))
        total = None
        for p in range(PAIRS):
            q_real, q_imag = qr_ref[p], qi_ref[p]
            real, imag = combine(product3(left_rows(q_real, q_imag), right_blocks(sr_ref[p], si_ref[p])))
            real, imag = weighted(n, p, q_real + real, q_imag + imag)
            total = (real, imag) if total is None else (total[0] + real, total[1] + imag)
        tr_ref[n], ti_ref[n] = total

    tr_ref[...] = t1r_ref[...]
    ti_ref[...] = t1i_ref[...]

    def one_freq(n, carry):
        owner = (x + XS - n // PER_FREQ) % XS
        count = n_ref[owner * (PER_FREQ * LINE) + t * PER_FREQ + n % PER_FREQ]
        pl.when(count == 2)(functools.partial(two_steps, n))
        pl.when(count == 3)(functools.partial(three_steps, n))
        return carry

    lax.fori_loop(0, N_LOCAL, one_freq, 0)

    quarter = lanes % NORB // (NORB // YS)
    for n_high in range(2):
        mixed = [None] * YS
        for n_low in range(4):
            n = (x + XS - n_high * 2 - n_low // 2) % XS * PER_FREQ + n_low % 2
            g = g_ref[n]
            turned = jnp.where(first, -swap(g), swap(g))
            r_high, r_low = halves(jnp.concatenate([g, g, turned, turned], 0))
            l_high, l_low = halves(jnp.concatenate([tr_ref[n], ti_ref[n]], 1))
            both = dot(l_high, jnp.concatenate([r_high, r_low], 1))
            value = both[:, :WIDE] + both[:, WIDE:] + dot(l_low, r_high)
            for to_y in range(YS):
                shift = (n_low - to_y) * (NORB // YS) % WIDE
                moved = pltpu.roll(value, shift, 1) if shift else value
                mixed[to_y] = moved if n_low == 0 else jnp.where(quarter == n_low, moved, mixed[to_y])
        for to_y in range(YS):
            for to_x in range(XS):
                out_ref[to_x, to_y, n_high] = mixed[to_y][to_x * LINE : (to_x + 1) * LINE]


def invert(counts, *gathered):
    slots = pltpu.VMEM((PAIRS, NORB, WIDE), F32)
    totals = pltpu.VMEM((N_LOCAL, NORB, WIDE), F32)
    return pl.pallas_call(
        power_kernel,
        name="invert",
        out_shape=jax.ShapeDtypeStruct((XS, YS, 2, LINE, WIDE), F32),
        in_specs=[smem()] + [vmem()] * 7,
        out_specs=vmem(),
        scratch_shapes=[slots] * 4 + [totals] * 2,
        compiler_params=pltpu.CompilerParams(vmem_limit_bytes=16 << 20),
    )(counts, *gathered)


def exit_kernel(o_ref, q_ref, landed, rows_ref, as_, ar, bs, br):
    f = lax.axis_index("freq")
    y = lax.axis_index("kgrp")
    x, t = f // LINE, f % LINE
    z, c = t // CORES, t % CORES
    plane = [(dx, dy) for dx in range(XS) for dy in range(YS) if dx or dy]
    line = [(dz, dc) for dz in range(ZS) for dc in range(CORES) if dz or dc]

    def in_plane(dx, dy):
        return {"freq": (x + dx) % XS * LINE + t, "kgrp": (y + dy) % YS}

    def place(dz, dc):
        return (z + dz) % ZS * CORES + (c + dc) % CORES

    greet([in_plane(*d) for d in plane] + [on_freq(x * LINE + place(*d)) for d in line])
    started = []
    for dx, dy in plane:
        slot = dx * YS + dy
        copy = send(
            o_ref.at[(x + dx) % XS, (y + dy) % YS], landed.at[slot], as_.at[slot], ar.at[slot], in_plane(dx, dy)
        )
        copy.start()
        started.append(copy)
    total = o_ref[x, y]
    for dx, dy in plane:
        slot = dx * YS + dy
        send(o_ref.at[x, y], landed.at[slot], as_.at[slot], ar.at[slot], in_plane(dx, dy)).wait_recv()
        total = total + landed[slot]
    for to in range(LINE):
        for n_high in range(2):
            rows_ref[to, n_high : n_high + 1] = total[n_high, to : to + 1]
    for dz, dc in line:
        slot = dz * CORES + dc
        to = place(dz, dc)
        copy = send(rows_ref.at[to], q_ref.at[t], bs.at[slot], br.at[slot], on_freq(x * LINE + to))
        copy.start()
        started.append(copy)
    q_ref[pl.ds(t, 1)] = rows_ref[pl.ds(t, 1)]
    for dz, dc in line:
        slot = dz * CORES + dc
        source = (z + ZS - dz) % ZS * CORES + (c + CORES - dc) % CORES
        send(rows_ref.at[source], q_ref.at[source], bs.at[slot], br.at[slot], on_freq(x * LINE + place(dz, dc))).wait_recv()
    for copy in started:
        copy.wait_send()


def leave(sums):
    dma = pltpu.SemaphoreType.DMA
    return pl.pallas_call(
        exit_kernel,
        name="leave",
        out_shape=jax.ShapeDtypeStruct((LINE, 2, WIDE), F32),
        in_specs=[vmem()],
        out_specs=vmem(),
        scratch_shapes=[
            pltpu.VMEM((XS * YS, 2, LINE, WIDE), F32),
            pltpu.VMEM((LINE, 2, WIDE), F32),
            dma((XS * YS,)),
            dma((XS * YS,)),
            dma((LINE,)),
            dma((LINE,)),
        ],
        compiler_params=pltpu.CompilerParams(
            collective_id=1, has_side_effects=True, vmem_limit_bytes=8 << 20
        ),
    )(sums)


def per_device(hamiltonian, self_energy, guess_factor, weights, counts):
    gathered = gather(weights, hamiltonian, self_energy, guess_factor)
    sums = invert(counts, *gathered)
    arrived = leave(sums)
    pieces = arrived.reshape(LINE, 2, 2, 2, 2, NORB // YS)
    return pieces.transpose(5, 2, 1, 3, 0, 4).reshape(NORB // YS, 2 * FREQ)


def solution(mesh):
    return jax.shard_map(
        per_device,
        mesh=mesh,
        in_specs=(
            P(("freq", "kgrp"), None, None),
            P("freq", None, None),
            P("freq", None, None),
            P(),
            P(),
        ),
        out_specs=P(("freq", "kgrp"), None),
        check_vma=False,
    )
```

time: 65.5 us -> 50.8 us (0.78); the launches traced: 64.2 us -> 50.5 us
  Pallas kernels: 62.5 us -> 45.7 us
  local copies, waits for them, and re-layouts: 1.66 us -> 4.71 us
    pallas_call x2, Pallas kernels: 39.2 us -> 27.1 us  [the longest x1 23.1 us: gather(): pl.pallas_call(gather_kernel, name='gather', out_shape=(totals, powers, p...]
    pallas_call x1, Pallas kernels: 23.3 us -> 18.7 us  [leave(): pl.pallas_call(exit_kernel, name='leave', out_shape=jax.ShapeDtypeStruct(...]
    unnamed x0 -> x10, local copies, waits for them, and re-layouts: none -> 3.76 us
    reshape x2, local copies, waits for them, and re-layouts: 0.98 us -> 0.27 us  [per_device(): pieces = arrived.reshape(LINE, 2, 2, 2, 2, NORB // YS)]
where the time goes in v2:
time: 50.8 us; the launch traced here: 50.5 us
  Pallas kernels  45.7 us (90%)
  local copies, waits for them, and re-layouts  4.71 us (9%)
    pallas_call x1, Pallas kernels, gather(): pl.pallas_call(gather_kernel, name='gather', out_shape=(totals, powers, p...  23.1 us
    pallas_call x1, Pallas kernels, leave(): pl.pallas_call(exit_kernel, name='leave', out_shape=jax.ShapeDtypeStruct(...  18.7 us
    pallas_call x1, Pallas kernels, invert(): pl.pallas_call(power_kernel, name='invert', out_shape=jax.ShapeDtypeStruc...  3.93 us
    unnamed x10, local copies, waits for them, and re-layouts  3.76 us

profile of v2, /device:TPU:1, one launch (start us, length us, event | category | flops | bytes accessed | tf_op | source)
XLA Modules:
  0.0 50.5 jit_solution(10652856385259189847)
XLA Ops:
  0.0 0.0 copy-start
  0.0 0.8 %copy-done = f32[2,64,128]{2,1,0:T(8,128)S(1)} copy-done((f32[2,64,128]{2,1,0:T(8,128)S(1)}, f32[2,64,128]{2,1,0:T(8,128)}, u32[]{:S(2)}) %copy-start) | copy-done | bytes 65560
  0.8 0.0 copy-start.1
  0.8 0.8 %copy-done.1 = f32[2,64,128]{2,1,0:T(8,128)S(1)} copy-done((f32[2,64,128]{2,1,0:T(8,128)S(1)}, f32[2,64,128]{2,1,0:T(8,128)}, u32[]{:S(2)}) %copy-start.1) | copy-done | bytes 65560
  1.7 0.0 copy-start.2
  1.7 0.8 %copy-done.2 = f32[1,64,128]{2,1,0:T(8,128)S(1)} copy-done((f32[1,64,128]{2,1,0:T(8,128)S(1)}, f32[1,64,128]{2,1,0:T(8,128)}, u32[]{:S(2)}) %copy-start.2) | copy-done | bytes 32792
  2.4 0.0 copy-start.3
  2.4 0.7 %copy-done.3 = s32[256]{0:T(256)S(1)} copy-done((s32[256]{0:T(256)S(1)}, s32[256]{0:T(256)}, u32[]{:S(2)}) %copy-start.3) | copy-done | bytes 1048
  3.1 23.1 %gather.1 = (f32[8,64,128]{2,1,0:T(8,128)S(1)}, f32[8,8,64,128]{3,2,1,0:T(8,128)S(1)}, f32[8,8,64,128]{3,2,1,0:T(8,128)S(1)}, f32[8,8,128]{2,1,0:T(8,128)S(1)}, ...) custom-call(s32[256]{0:T(256)S(1)} %copy-done.3, f32[1,64,128]{2,1,0:T(8,128)S(1)} %copy-done.2, ...), custom_call_target="tpu_custom_call" | custom-call | tf_op jit(solution)/shard_map/gather/pallas_call | solution.py:262
  26.2 0.0 copy-start.4
  26.3 0.6 %copy-done.4 = s32[128]{0:T(128)S(1)} copy-done((s32[128]{0:T(128)S(1)}, s32[128]{0:T(128)}, u32[]{:S(2)}) %copy-start.4) | copy-done | bytes 536
  26.9 3.9 %invert.1.o_ref = f32[4,4,2,16,128]{4,3,2,1,0:T(8,128)S(1)} custom-call(s32[128]{0:T(128)S(1)} %copy-done.4, f32[8,64,128]{2,1,0:T(8,128)S(1)} %get-tuple-element.12.g_ref, f32[8,8,64,128]{3,2,1,0:T(8,128)S(1)} %get-tuple-element.13.er_ref, f32[8,8,64,128]{3,2,1,0:T(8,128)S(1)} %get-tuple-element.14.ei_ref, f32[8,8,128]{2,1,0:T(8,128)S(1)} %get-tuple-element.15.ur_ref, ...), custom_call_target="tpu_custom_call" | custom-call | tf_op jit(solution)/shard_map/invert/pallas_call | solution.py:387
  30.8 18.7 %leave.1 = f32[16,2,128]{2,1,0:T(2,128)S(1)} custom-call(f32[4,4,2,16,128]{4,3,2,1,0:T(8,128)S(1)} %invert.1.o_ref), custom_call_target="tpu_custom_call" | custom-call | tf_op jit(solution)/shard_map/leave/pallas_call | solution.py:446
  49.5 0.2 reshape.6
  49.8 0.7 %copy.8 = f32[16,256]{1,0:T(8,128)} copy(f32[16,256]{0,1:T(8,128)S(1)} %bitcast.3) | data formatting | bytes 32768 | tf_op jit(solution)/shard_map/reshape | solution.py:471
  (1 shorter events, 0.0 us)
Async XLA Ops:
  0.0 0.8 %copy-start = (f32[2,64,128]{2,1,0:T(8,128)S(1)}, f32[2,64,128]{2,1,0:T(8,128)}, u32[]{:S(2)}) copy-start(f32[2,64,128]{2,1,0:T(8,128)} %s_ref.1) | copy-start | bytes 196612
  0.8 0.8 %copy-start.1 = (f32[2,64,128]{2,1,0:T(8,128)S(1)}, f32[2,64,128]{2,1,0:T(8,128)}, u32[]{:S(2)}) copy-start(f32[2,64,128]{2,1,0:T(8,128)} %g_ref.1) | copy-start | bytes 196612
  1.7 0.8 %copy-start.2 = (f32[1,64,128]{2,1,0:T(8,128)S(1)}, f32[1,64,128]{2,1,0:T(8,128)}, u32[]{:S(2)}) copy-start(f32[1,64,128]{2,1,0:T(8,128)} %h_ref.1) | copy-start | bytes 98308
  2.4 0.7 %copy-start.3 = (s32[256]{0:T(256)S(1)}, s32[256]{0:T(256)}, u32[]{:S(2)}) copy-start(s32[256]{0:T(256)} %w_ref.1) | copy-start | bytes 3076
  26.2 0.7 %copy-start.4 = (s32[128]{0:T(128)S(1)}, s32[128]{0:T(128)}, u32[]{:S(2)}) copy-start(s32[128]{0:T(128)} %n_ref.1) | copy-start | bytes 1540

commit v3 on v2

--- a/solution.py
+++ b/solution.py
@@ -31,6 +31,10 @@
     return pl.BlockSpec(memory_space=pltpu.SMEM)
 
 
+def hbm():
+    return pl.BlockSpec(memory_space=pltpu.HBM)
+
+
 def on_freq(index):
     return {"freq": index}
 
@@ -39,7 +43,7 @@
     barrier = pltpu.get_barrier_semaphore()
     for target in targets:
         pl.semaphore_signal(barrier, inc=1, device_id=target, device_id_type=pl.DeviceIdType.MESH)
-    pl.semaphore_wait(barrier, len(targets))
+    return lambda: pl.semaphore_wait(barrier, len(targets))
 
 
 def send(src, dst, send_sem, recv_sem, target):
@@ -54,6 +58,7 @@
 
 
 Z_ORDER = (4, 3, 5, 2, 6, 1, 7)
+SLOT_DX = (0, 1, 3, 2)
 
 
 def halves(value):
@@ -85,10 +90,10 @@
 
 
 def gather_kernel(
-    w_ref, h_ref, s_ref, g_ref,
-    gall, er_ref, ei_ref, ur_ref, ui_ref, tr_ref, ti_ref,
-    hall, sall, wh, wl, hcol, hrow, gcat, gz, zcol, zrow, gh_ref,
-    zs, zr, ps, pr, ss, sr, gs, gr,
+    w_hbm, n_hbm, h_hbm, s_hbm, g_hbm,
+    gall, er_ref, ei_ref, ur_ref, ui_ref, tr_ref, ti_ref, count_ref,
+    w_ref, n_ref, hall, sall, wh, wl, hcol, hrow, gcat, gz, zcol, zrow, gh_ref,
+    zs, zr, ps, pr, ss, sr, gs, gr, own,
 ):
     f = lax.axis_index("freq")
     y = lax.axis_index("kgrp")
@@ -124,13 +129,13 @@
     def diagonal_row(value):
         return jnp.sum(jnp.where(eye_mask, value, 0.0), 0, keepdims=True)
 
-    def prepare_freqs(dx):
-        owner = (x + XS - dx) % XS
+    def prepare_freqs(slot):
+        owner = (x + XS - SLOT_DX[slot]) % XS
         for b in range(PER_FREQ):
-            n = dx * PER_FREQ + b
-            matsubara = (2 * (owner * (PER_FREQ * LINE) + t * PER_FREQ + b) + 1).astype(F32) * (
-                math.pi / (2 * FREQ)
-            )
+            n = slot * PER_FREQ + b
+            freq_id = owner * (PER_FREQ * LINE) + t * PER_FREQ + b
+            count_ref[n : n + 1] = jnp.full((1, WIDE), n_ref[freq_id].astype(F32))
+            matsubara = (2 * freq_id + 1).astype(F32) * (math.pi / (2 * FREQ))
             shift = jnp.where(first, chem_potential, matsubara)
             zed = jnp.where(eye_mask, shift, 0.0) - sall[n]
             real, imag = paired(zed, zed)
@@ -148,17 +153,23 @@
         hcol[p] = diagonal_columns(real)
         hrow[p : p + 1] = diagonal_row(real)
 
-    def signal_all(targets):
-        barrier = pltpu.get_barrier_semaphore()
-        for target in targets:
-            pl.semaphore_signal(barrier, inc=1, device_id=target, device_id_type=pl.DeviceIdType.MESH)
-        return barrier
-
-    greeted = [partner] + [along_z(dz) for dz in range(1, ZS)] + [along_x(dx) for dx in range(1, XS)]
-    barrier = signal_all(greeted)
-    hall[0, 0] = h_ref[0]
-    sall[:PER_FREQ] = s_ref[...]
-    gall[:PER_FREQ] = g_ref[...]
+    first_rows = pl.ds(0, PER_FREQ)
+    own_h, own_s, own_g = hall.at[0, 0], sall.at[first_rows], gall.at[first_rows]
+    loads = [
+        pltpu.make_async_copy(src, dst, own.at[i])
+        for i, (src, dst) in enumerate(
+            ((h_hbm.at[0], own_h), (g_hbm, own_g), (s_hbm, own_s), (w_hbm, w_ref), (n_hbm, n_ref))
+        )
+    ]
+    for load in loads:
+        load.start()
+    await_greetings = greet(
+        [partner] + [along_z(dz) for dz in range(1, ZS)] + [along_x(dx) for dx in range(1, XS)]
+    )
+    tr_ref[...] = jnp.zeros_like(tr_ref)
+    ti_ref[...] = jnp.zeros_like(ti_ref)
+    for load in loads:
+        load.wait()
     prepare_freqs(0)
 
     def add_up(i, total):
@@ -167,73 +178,52 @@
         return total
 
     inv_total = 1.0 / lax.fori_loop(0, KPTS // 16, add_up, jnp.int32(0)).astype(F32)
-    tr_ref[...] = jnp.zeros_like(tr_ref)
-    ti_ref[...] = jnp.zeros_like(ti_ref)
-    pl.semaphore_wait(barrier, len(greeted))
+    await_greetings()
+
+    def z_copy(dz):
+        return send(own_h, hall.at[dz, 0], zs.at[dz], zr.at[dz], along_z(dz))
+
+    def partner_copy(dz):
+        return send(hall.at[dz, 0], hall.at[dz, 1], ps.at[dz], pr.at[dz], partner)
+
+    def freq_copies(slot):
+        rows = pl.ds(slot * PER_FREQ, PER_FREQ)
+        target = along_x(SLOT_DX[slot])
+        return (
+            send(own_g, gall.at[rows], gs.at[slot], gr.at[slot], target),
+            send(own_s, sall.at[rows], ss.at[slot], sr.at[slot], target),
+        )
 
     started = []
-    for dz in Z_ORDER:
-        copy = send(h_ref.at[0], hall.at[dz, 0], zs.at[dz], zr.at[dz], along_z(dz))
+
+    def begin(copy):
         copy.start()
         started.append(copy)
-    copy = send(h_ref.at[0], hall.at[0, 1], ps.at[0], pr.at[0], partner)
-    copy.start()
-    started.append(copy)
-
-    def freq_copies(dx):
-        rows = pl.ds(dx * PER_FREQ, PER_FREQ)
-        return (
-            send(g_ref, gall.at[rows], gs.at[dx], gr.at[dx], along_x(dx)),
-            send(s_ref, sall.at[rows], ss.at[dx], sr.at[dx], along_x(dx)),
+
+    begin(partner_copy(0))
+    for dz in Z_ORDER:
+        begin(z_copy(dz))
+    for slot in (3, 1, 2):
+        for copy in freq_copies(slot):
+            begin(copy)
+
+    def residuals(p, low, high):
+        left = gcat[low:high].reshape((high - low) * NORB, 2 * WIDE)
+        right = wh[p]
+        gh_ref[: (high - low) * NORB] = dot(left, jnp.concatenate([right, right], 0)) + dot(
+            left[:, :WIDE], wl[p]
         )
-
-    for dx in (2, 1, 3):
-        for copy in freq_copies(dx):
-            copy.start()
-            started.append(copy)
-
-    def arrived_z(dz):
-        send(h_ref.at[0], hall.at[dz, 0], zs.at[dz], zr.at[dz], along_z(dz)).wait_recv()
-        copy = send(hall.at[dz, 0], hall.at[dz, 1], ps.at[dz], pr.at[dz], partner)
-        copy.start()
-        started.append(copy)
-
-    def arrived_x(dx):
-        for copy in freq_copies(dx):
-            copy.wait_recv()
-        prepare_freqs(dx)
-
-    def arrived_partner(dz):
-        send(h_ref.at[0], hall.at[dz, 1], ps.at[dz], pr.at[dz], partner).wait_recv()
-        prepare_pair(dz)
-
-    for dz in (1, 7, 2, 6):
-        arrived_z(dz)
-    arrived_partner(0)
-    arrived_x(1)
-    for dz in (3, 5):
-        arrived_z(dz)
-    arrived_x(3)
-    arrived_z(4)
-    arrived_x(2)
-    for dz in (1, 7, 2, 6, 3, 5, 4):
-        arrived_partner(dz)
-
-    def residual_pair(p, carry):
-        left = gcat[...].reshape(N_LOCAL * NORB, 2 * WIDE)
-        high = wh[p]
-        gh_ref[...] = dot(left, jnp.concatenate([high, high], 0)) + dot(left[:, :WIDE], wl[p])
         h_diag = hcol[p]
         chip = x * LINE + (z + ZS - p) % ZS * CORES
         w_one = w_ref[(chip + c) * YS + y].astype(F32) * inv_total
         w_two = w_ref[(chip + 1 - c) * YS + y].astype(F32) * inv_total
-        weight = jnp.where(first[:N_LOCAL], w_one, w_two)
-        d_real, d_imag = zrow[:, :WIDE] - hrow[pl.ds(p, 1)], zrow[:, WIDE:]
+        weight = jnp.where(first[: high - low], w_one, w_two)
+        d_real, d_imag = zrow[low:high, :WIDE] - hrow[pl.ds(p, 1)], zrow[low:high, WIDE:]
         inv = weight / (d_real * d_real + d_imag * d_imag)
-        ur_ref[p] = d_real * inv
-        ui_ref[p] = -d_imag * inv
-        for n in range(N_LOCAL):
-            a = gz[n] - gh_ref[n * NORB : (n + 1) * NORB]
+        ur_ref[p, low:high] = d_real * inv
+        ui_ref[p, low:high] = -d_imag * inv
+        for n in range(low, high):
+            a = gz[n] - gh_ref[(n - low) * NORB : (n - low + 1) * NORB]
             a_real, a_imag = a[:, :WIDE], a[:, WIDE:]
             d = zcol[n]
             d_real, d_imag = d[:, :WIDE] - h_diag, d[:, WIDE:]
@@ -247,25 +237,65 @@
             q_real = eye + e_real
             tr_ref[n] += q_real * u_real - e_imag * u_imag
             ti_ref[n] += q_real * u_imag + e_imag * u_real
-        return carry
-
-    lax.fori_loop(0, PAIRS, residual_pair, 0)
+
+    def residuals_of_all(low, high):
+        def body(p, carry):
+            residuals(p, low, high)
+            return carry
+
+        lax.fori_loop(0, PAIRS, body, 0, unroll=2)
+
+    def arrived_z(*steps):
+        for dz in steps:
+            z_copy(dz).wait_recv()
+            begin(partner_copy(dz))
+
+    def arrived_x(*slots):
+        for slot in slots:
+            for copy in freq_copies(slot):
+                copy.wait_recv()
+        for slot in slots:
+            prepare_freqs(slot)
+
+    def arrived_pair(*steps):
+        for dz in steps:
+            partner_copy(dz).wait_recv()
+        for dz in steps:
+            prepare_pair(dz)
+        for dz in steps:
+            residuals(dz, 0, PER_FREQ)
+
+    arrived_pair(0)
+    arrived_z(1, 7, 2, 6)
+    arrived_pair(1, 7)
+    arrived_z(3, 5)
+    arrived_pair(2, 6)
+    arrived_z(4)
+    arrived_x(1, 2)
+    arrived_pair(3, 5)
+    arrived_pair(4)
+    residuals_of_all(PER_FREQ, 3 * PER_FREQ)
+    arrived_x(3)
+    residuals_of_all(3 * PER_FREQ, N_LOCAL)
     for copy in started:
         copy.wait_send()
 
 
-def gather(weights, hamiltonian, self_energy, guess_factor):
+def gather(*values):
     dma = pltpu.SemaphoreType.DMA
     powers = jax.ShapeDtypeStruct((N_LOCAL, PAIRS, NORB, WIDE), F32)
     scales = jax.ShapeDtypeStruct((PAIRS, N_LOCAL, WIDE), F32)
     totals = jax.ShapeDtypeStruct((N_LOCAL, NORB, WIDE), F32)
+    counted = jax.ShapeDtypeStruct((N_LOCAL, WIDE), F32)
     return pl.pallas_call(
         gather_kernel,
         name="gather",
-        out_shape=(totals, powers, powers, scales, scales, totals, totals),
-        in_specs=[smem()] + [vmem()] * 3,
-        out_specs=(vmem(),) * 7,
+        out_shape=(totals, powers, powers, scales, scales, totals, totals, counted),
+        in_specs=[hbm()] * 5,
+        out_specs=(vmem(),) * 8,
         scratch_shapes=[
+            pltpu.SMEM((KPTS,), jnp.int32),
+            pltpu.SMEM((FREQ,), jnp.int32),
             pltpu.VMEM((ZS, CORES, NORB, WIDE), F32),
             pltpu.VMEM((N_LOCAL, NORB, WIDE), F32),
             pltpu.VMEM((PAIRS, WIDE, 2 * WIDE), BF),
@@ -279,17 +309,18 @@
             pltpu.VMEM((N_LOCAL * NORB, 2 * WIDE), F32),
         ]
         + [dma((ZS,))] * 4
-        + [dma((XS,))] * 4,
+        + [dma((XS,))] * 4
+        + [dma((5,))],
         compiler_params=pltpu.CompilerParams(
             collective_id=0, has_side_effects=True, vmem_limit_bytes=20 << 20
         ),
-    )(weights, hamiltonian, self_energy, guess_factor)
-
-
-def power_kernel(n_ref, g_ref, er_ref, ei_ref, ur_ref, ui_ref, t1r_ref, t1i_ref, out_ref, sr_ref, si_ref, qr_ref, qi_ref, tr_ref, ti_ref):
-    f = lax.axis_index("freq")
-    x, t = f // LINE, f % LINE
-    lanes, first, eye_mask = lane_masks()
+    )(*(pltpu.with_memory_space_constraint(value, pltpu.HBM) for value in values))
+
+
+def power_kernel(
+    er_ref, ei_ref, ur_ref, ui_ref, t1r_ref, t1i_ref, count_ref, tr_ref, ti_ref, sr_ref, si_ref, qr_ref, qi_ref, steps_ref
+):
+    _, first, eye_mask = lane_masks()
     eye = eye_mask.astype(F32)
     first_bf = first.astype(F32).astype(BF)
     second_bf = (1.0 - first.astype(F32)).astype(BF)
@@ -349,23 +380,56 @@
             total = (real, imag) if total is None else (total[0] + real, total[1] + imag)
         tr_ref[n], ti_ref[n] = total
 
+    for n in range(N_LOCAL):
+        steps_ref[n] = jnp.max(count_ref[n : n + 1])
     tr_ref[...] = t1r_ref[...]
     ti_ref[...] = t1i_ref[...]
 
     def one_freq(n, carry):
-        owner = (x + XS - n // PER_FREQ) % XS
-        count = n_ref[owner * (PER_FREQ * LINE) + t * PER_FREQ + n % PER_FREQ]
-        pl.when(count == 2)(functools.partial(two_steps, n))
-        pl.when(count == 3)(functools.partial(three_steps, n))
+        steps = steps_ref[n]
+        pl.when((steps > 1.5) & (steps < 2.5))(functools.partial(two_steps, n))
+        pl.when(steps > 2.5)(functools.partial(three_steps, n))
         return carry
 
     lax.fori_loop(0, N_LOCAL, one_freq, 0)
 
+
+def invert(*gathered):
+    slots = pltpu.VMEM((PAIRS, NORB, WIDE), F32)
+    totals = jax.ShapeDtypeStruct((N_LOCAL, NORB, WIDE), F32)
+    return pl.pallas_call(
+        power_kernel,
+        name="invert",
+        out_shape=(totals, totals),
+        in_specs=[vmem()] * 7,
+        out_specs=(vmem(),) * 2,
+        scratch_shapes=[slots] * 4 + [pltpu.SMEM((N_LOCAL,), F32)],
+        compiler_params=pltpu.CompilerParams(vmem_limit_bytes=16 << 20),
+    )(*gathered)
+
+
+def exit_kernel(g_ref, tr_ref, ti_ref, q_ref, o_ref, landed, rows_ref, as_, ar, bs, br):
+    f = lax.axis_index("freq")
+    y = lax.axis_index("kgrp")
+    x, t = f // LINE, f % LINE
+    z, c = t // CORES, t % CORES
+    plane = [(dx, dy) for dx in range(XS) for dy in range(YS) if dx or dy]
+    line = [(dz, dc) for dz in range(ZS) for dc in range(CORES) if dz or dc]
+
+    def in_plane(dx, dy):
+        return {"freq": (x + dx) % XS * LINE + t, "kgrp": (y + dy) % YS}
+
+    def place(dz, dc):
+        return (z + dz) % ZS * CORES + (c + dc) % CORES
+
+    await_greetings = greet([in_plane(*d) for d in plane] + [on_freq(x * LINE + place(*d)) for d in line])
+    lanes, first, _ = lane_masks()
     quarter = lanes % NORB // (NORB // YS)
     for n_high in range(2):
         mixed = [None] * YS
         for n_low in range(4):
-            n = (x + XS - n_high * 2 - n_low // 2) % XS * PER_FREQ + n_low % 2
+            dx = (x + XS - n_high * 2 - n_low // 2) % XS
+            n = (dx + dx // 2 * (5 - 2 * dx)) * PER_FREQ + n_low % 2
             g = g_ref[n]
             turned = jnp.where(first, -swap(g), swap(g))
             r_high, r_low = halves(jnp.concatenate([g, g, turned, turned], 0))
@@ -378,38 +442,8 @@
                 mixed[to_y] = moved if n_low == 0 else jnp.where(quarter == n_low, moved, mixed[to_y])
         for to_y in range(YS):
             for to_x in range(XS):
-                out_ref[to_x, to_y, n_high] = mixed[to_y][to_x * LINE : (to_x + 1) * LINE]
-
-
-def invert(counts, *gathered):
-    slots = pltpu.VMEM((PAIRS, NORB, WIDE), F32)
-    totals = pltpu.VMEM((N_LOCAL, NORB, WIDE), F32)
-    return pl.pallas_call(
-        power_kernel,
-        name="invert",
-        out_shape=jax.ShapeDtypeStruct((XS, YS, 2, LINE, WIDE), F32),
-        in_specs=[smem()] + [vmem()] * 7,
-        out_specs=vmem(),
-        scratch_shapes=[slots] * 4 + [totals] * 2,
-        compiler_params=pltpu.CompilerParams(vmem_limit_bytes=16 << 20),
-    )(counts, *gathered)
-
-
-def exit_kernel(o_ref, q_ref, landed, rows_ref, as_, ar, bs, br):
-    f = lax.axis_index("freq")
-    y = lax.axis_index("kgrp")
-    x, t = f // LINE, f % LINE
-    z, c = t // CORES, t % CORES
-    plane = [(dx, dy) for dx in range(XS) for dy in range(YS) if dx or dy]
-    line = [(dz, dc) for dz in range(ZS) for dc in range(CORES) if dz or dc]
-
-    def in_plane(dx, dy):
-        return {"freq": (x + dx) % XS * LINE + t, "kgrp": (y + dy) % YS}
-
-    def place(dz, dc):
-        return (z + dz) % ZS * CORES + (c + dc) % CORES
-
-    greet([in_plane(*d) for d in plane] + [on_freq(x * LINE + place(*d)) for d in line])
+                o_ref[to_x, to_y, n_high] = mixed[to_y][to_x * LINE : (to_x + 1) * LINE]
+    await_greetings()
     started = []
     for dx, dy in plane:
         slot = dx * YS + dy
@@ -441,15 +475,16 @@
         copy.wait_send()
 
 
-def leave(sums):
+def leave(*parts):
     dma = pltpu.SemaphoreType.DMA
     return pl.pallas_call(
         exit_kernel,
         name="leave",
         out_shape=jax.ShapeDtypeStruct((LINE, 2, WIDE), F32),
-        in_specs=[vmem()],
+        in_specs=[vmem()] * 3,
         out_specs=vmem(),
         scratch_shapes=[
+            pltpu.VMEM((XS, YS, 2, LINE, WIDE), F32),
             pltpu.VMEM((XS * YS, 2, LINE, WIDE), F32),
             pltpu.VMEM((LINE, 2, WIDE), F32),
             dma((XS * YS,)),
@@ -460,13 +495,12 @@
         compiler_params=pltpu.CompilerParams(
             collective_id=1, has_side_effects=True, vmem_limit_bytes=8 << 20
         ),
-    )(sums)
+    )(*parts)
 
 
 def per_device(hamiltonian, self_energy, guess_factor, weights, counts):
-    gathered = gather(weights, hamiltonian, self_energy, guess_factor)
-    sums = invert(counts, *gathered)
-    arrived = leave(sums)
+    g_all, *gathered = gather(weights, counts, hamiltonian, self_energy, guess_factor)
+    arrived = leave(g_all, *invert(*gathered))
     pieces = arrived.reshape(LINE, 2, 2, 2, 2, NORB // YS)
     return pieces.transpose(5, 2, 1, 3, 0, 4).reshape(NORB // YS, 2 * FREQ)
 

time: 50.8 us -> 45.3 us (0.89)
  local copies, waits for them, and re-layouts: 4.71 us -> 0.95 us
  Pallas kernels: 45.7 us -> 44 us
    unnamed x10 -> x0, local copies, waits for them, and re-layouts: 3.76 us -> none
    pallas_call x1, Pallas kernels: 18.7 us -> 17.6 us  [leave(): pl.pallas_call(exit_kernel, name='leave', out_shape=jax.ShapeDtypeStruct(...]
where the time goes in v3:
time: 45.3 us; the launch traced here: 44.9 us
  Pallas kernels  44 us (97%)
  local copies, waits for them, and re-layouts  0.95 us (2%)
    pallas_call x1, Pallas kernels, gather(): pl.pallas_call(gather_kernel, name='gather', out_shape=(totals, powers, p...  22.8 us
    pallas_call x1, Pallas kernels, leave(): pl.pallas_call(exit_kernel, name='leave', out_shape=jax.ShapeDtypeStruct(...  17.6 us
    pallas_call x1, Pallas kernels, invert(): pl.pallas_call(power_kernel, name='invert', out_shape=(totals, totals), i...  3.6 us

profile of v3, /device:TPU:1, one launch (start us, length us, event | category | flops | bytes accessed | tf_op | source)
XLA Modules:
  0.0 44.9 jit_solution(2690160885985704269)
XLA Ops:
  0.0 22.8 %gather.1 = (f32[8,64,128]{2,1,0:T(8,128)S(1)}, f32[8,8,64,128]{3,2,1,0:T(8,128)S(1)}, f32[8,8,64,128]{3,2,1,0:T(8,128)S(1)}, f32[8,8,128]{2,1,0:T(8,128)S(1)}, ...) custom-call(s32[256]{0:T(256)} %w_hbm.1, s32[128]{0:T(128)} %n_hbm.1, ...), custom_call_target="tpu_custom_call" | custom-call | tf_op jit(solution)/shard_map/gather/pallas_call | solution.py:290
  22.8 3.6 %invert.1 = (f32[8,64,128]{2,1,0:T(8,128)S(1)}, f32[8,64,128]{2,1,0:T(8,128)S(1)}) custom-call(f32[8,8,64,128]{3,2,1,0:T(8,128)S(1)} %get-tuple-element.16.er_ref, f32[8,8,64,128]{3,2,1,0:T(8,128)S(1)} %get-tuple-element.17.ei_ref, f32[8,8,128]{2,1,0:T(8,128)S(1)} %get-tuple-element.18.ur_ref, f32[8,8,128]{2,1,0:T(8,128)S(1)} %get-tuple-element.19.ui_ref, ...), custom_call_target="tpu_custom_call" | custom-call | tf_op jit(solution)/shard_map/invert/pallas_call | solution.py:400
  26.4 17.6 %leave.1 = f32[16,2,128]{2,1,0:T(2,128)S(1)} custom-call(f32[8,64,128]{2,1,0:T(8,128)S(1)} %get-tuple-element.15.g_ref, f32[8,64,128]{2,1,0:T(8,128)S(1)} %get-tuple-element.23.tr_ref, f32[8,64,128]{2,1,0:T(8,128)S(1)} %get-tuple-element.24.ti_ref), custom_call_target="tpu_custom_call" | custom-call | tf_op jit(solution)/shard_map/leave/pallas_call | solution.py:480
  44.0 0.2 reshape.6
  44.3 0.7 %copy.8 = f32[16,256]{1,0:T(8,128)} copy(f32[16,256]{0,1:T(8,128)S(1)} %bitcast.3) | data formatting | bytes 32768 | tf_op jit(solution)/shard_map/reshape | solution.py:505
  (1 shorter events, 0.0 us)

commit v4 on v3

--- a/solution.py
+++ b/solution.py
@@ -92,7 +92,7 @@
 def gather_kernel(
     w_hbm, n_hbm, h_hbm, s_hbm, g_hbm,
     gall, er_ref, ei_ref, ur_ref, ui_ref, tr_ref, ti_ref, count_ref,
-    w_ref, n_ref, hall, sall, wh, wl, hcol, hrow, gcat, gz, zcol, zrow, gh_ref,
+    w_ref, n_ref, h_ref, hall, sall, wh, wl, hcol, hrow, gcat, gz, zcol, zrow, gh_ref,
     zs, zr, ps, pr, ss, sr, gs, gr, own,
 ):
     f = lax.axis_index("freq")
@@ -100,8 +100,11 @@
     x, t = f // LINE, f % LINE
     z, c = t // CORES, t % CORES
     partner = on_freq(x * LINE + z * CORES + (1 - c))
-    _, first, eye_mask = lane_masks()
+    lanes, first, eye_mask = lane_masks()
     eye = eye_mask.astype(F32)
+    half = NORB // 2
+    row_ids = lax.broadcasted_iota(jnp.int32, (NORB, WIDE), 0)
+    below, above = row_ids > lanes % NORB, row_ids < lanes % NORB
 
     def along_z(dz):
         return on_freq(x * LINE + (z + dz) % ZS * CORES + c)
@@ -146,7 +149,13 @@
             zrow[n : n + 1] = jnp.concatenate([diagonal_row(real), diagonal_row(imag)], 1)
 
     def prepare_pair(p):
-        real, imag = paired(hall[p, 0], hall[p, 1])
+        one, two = hall[p, 0], hall[p, 1]
+        packed = jnp.concatenate(
+            [jnp.where(first[:half], one, swap(two)), jnp.where(first[:half], swap(one), two)], 0
+        )
+        flipped = jnp.concatenate([packed, swap(packed)], 0).T[:NORB]
+        real = jnp.where(above, flipped, packed)
+        imag = jnp.where(above, packed, jnp.where(below, -flipped, 0.0))
         high, low = as_right(real, imag)
         wh[p] = high
         wl[p] = low
@@ -158,7 +167,7 @@
     loads = [
         pltpu.make_async_copy(src, dst, own.at[i])
         for i, (src, dst) in enumerate(
-            ((h_hbm.at[0], own_h), (g_hbm, own_g), (s_hbm, own_s), (w_hbm, w_ref), (n_hbm, n_ref))
+            ((h_hbm.at[0], h_ref), (g_hbm, own_g), (s_hbm, own_s), (w_hbm, w_ref), (n_hbm, n_ref))
         )
     ]
     for load in loads:
@@ -170,6 +179,9 @@
     ti_ref[...] = jnp.zeros_like(ti_ref)
     for load in loads:
         load.wait()
+    h = h_ref[...]
+    folded = jnp.where(above ^ first, h, swap(h))
+    own_h[...] = jnp.where(first[:half], folded[:half], folded[half:])
     prepare_freqs(0)
 
     def add_up(i, total):
@@ -188,10 +200,15 @@
 
     def freq_copies(slot):
         rows = pl.ds(slot * PER_FREQ, PER_FREQ)
-        target = along_x(SLOT_DX[slot])
+        if slot < 3:
+            g_from, s_from = own_g, own_s
+            g_to = s_to = along_x(SLOT_DX[slot])
+        else:
+            g_from, g_to = gall.at[pl.ds(1 * PER_FREQ, PER_FREQ)], along_x(1)
+            s_from, s_to = sall.at[pl.ds(2 * PER_FREQ, PER_FREQ)], along_x(XS - 1)
         return (
-            send(own_g, gall.at[rows], gs.at[slot], gr.at[slot], target),
-            send(own_s, sall.at[rows], ss.at[slot], sr.at[slot], target),
+            send(g_from, gall.at[rows], gs.at[slot], gr.at[slot], g_to),
+            send(s_from, sall.at[rows], ss.at[slot], sr.at[slot], s_to),
         )
 
     started = []
@@ -203,9 +220,10 @@
     begin(partner_copy(0))
     for dz in Z_ORDER:
         begin(z_copy(dz))
-    for slot in (3, 1, 2):
-        for copy in freq_copies(slot):
-            begin(copy)
+    begin(freq_copies(1)[0])
+    begin(freq_copies(2)[1])
+    begin(freq_copies(1)[1])
+    begin(freq_copies(2)[0])
 
     def residuals(p, low, high):
         left = gcat[low:high].reshape((high - low) * NORB, 2 * WIDE)
@@ -238,24 +256,10 @@
             tr_ref[n] += q_real * u_real - e_imag * u_imag
             ti_ref[n] += q_real * u_imag + e_imag * u_real
 
-    def residuals_of_all(low, high):
-        def body(p, carry):
-            residuals(p, low, high)
-            return carry
-
-        lax.fori_loop(0, PAIRS, body, 0, unroll=2)
-
     def arrived_z(*steps):
         for dz in steps:
             z_copy(dz).wait_recv()
             begin(partner_copy(dz))
-
-    def arrived_x(*slots):
-        for slot in slots:
-            for copy in freq_copies(slot):
-                copy.wait_recv()
-        for slot in slots:
-            prepare_freqs(slot)
 
     def arrived_pair(*steps):
         for dz in steps:
@@ -265,18 +269,43 @@
         for dz in steps:
             residuals(dz, 0, PER_FREQ)
 
+    near_g, near_s = freq_copies(1), freq_copies(2)
+    far = freq_copies(3)
     arrived_pair(0)
-    arrived_z(1, 7, 2, 6)
+    arrived_z(1, 7)
+    near_g[0].wait_recv()
+    begin(far[0])
+    near_s[1].wait_recv()
+    begin(far[1])
+    arrived_z(2, 6)
     arrived_pair(1, 7)
     arrived_z(3, 5)
     arrived_pair(2, 6)
+    near_g[1].wait_recv()
+    near_s[0].wait_recv()
+    prepare_freqs(1)
+    prepare_freqs(2)
     arrived_z(4)
-    arrived_x(1, 2)
     arrived_pair(3, 5)
+
+    def near_freqs(q, carry):
+        residuals(1 + q, PER_FREQ, 3 * PER_FREQ)
+        residuals(ZS - 1 - q, PER_FREQ, 3 * PER_FREQ)
+        return carry
+
+    lax.fori_loop(0, 3, near_freqs, 0)
     arrived_pair(4)
-    residuals_of_all(PER_FREQ, 3 * PER_FREQ)
-    arrived_x(3)
-    residuals_of_all(3 * PER_FREQ, N_LOCAL)
+    residuals(0, PER_FREQ, 3 * PER_FREQ)
+    residuals(4, PER_FREQ, 3 * PER_FREQ)
+    for copy in far:
+        copy.wait_recv()
+    prepare_freqs(3)
+
+    def far_freqs(p, carry):
+        residuals(p, 3 * PER_FREQ, N_LOCAL)
+        return carry
+
+    lax.fori_loop(0, PAIRS, far_freqs, 0, unroll=4)
     for copy in started:
         copy.wait_send()
 
@@ -296,7 +325,8 @@
         scratch_shapes=[
             pltpu.SMEM((KPTS,), jnp.int32),
             pltpu.SMEM((FREQ,), jnp.int32),
-            pltpu.VMEM((ZS, CORES, NORB, WIDE), F32),
+            pltpu.VMEM((NORB, WIDE), F32),
+            pltpu.VMEM((ZS, CORES, NORB // 2, WIDE), F32),
             pltpu.VMEM((N_LOCAL, NORB, WIDE), F32),
             pltpu.VMEM((PAIRS, WIDE, 2 * WIDE), BF),
             pltpu.VMEM((PAIRS, WIDE, 2 * WIDE), BF),

time: 45.3 us -> 42 us (0.927); the launches traced: 44.9 us -> 42.6 us
  Pallas kernels: 44 us -> 41.6 us
    pallas_call x1, Pallas kernels: 22.8 us -> 19.8 us  [gather(): pl.pallas_call(gather_kernel, name='gather', out_shape=(totals, powers, p...]
    pallas_call x1, Pallas kernels: 3.6 us -> 5.07 us  [invert(): pl.pallas_call(power_kernel, name='invert', out_shape=(totals, totals), i...]
    pallas_call x1, Pallas kernels: 17.6 us -> 16.7 us  [leave(): pl.pallas_call(exit_kernel, name='leave', out_shape=jax.ShapeDtypeStruct(...]
where the time goes in v4:
time: 42 us; the launch traced here: 42.6 us
  Pallas kernels  41.6 us (99%)
  local copies, waits for them, and re-layouts  0.95 us (2%)
    pallas_call x1, Pallas kernels, gather(): pl.pallas_call(gather_kernel, name='gather', out_shape=(totals, powers, p...  19.8 us
    pallas_call x1, Pallas kernels, leave(): pl.pallas_call(exit_kernel, name='leave', out_shape=jax.ShapeDtypeStruct(...  16.7 us
    pallas_call x1, Pallas kernels, invert(): pl.pallas_call(power_kernel, name='invert', out_shape=(totals, totals), i...  5.07 us

profile of v4, /device:TPU:1, one launch (start us, length us, event | category | flops | bytes accessed | tf_op | source)
XLA Modules:
  0.0 42.6 jit_solution(920413392754010597)
XLA Ops:
  0.0 19.8 %gather.1 = (f32[8,64,128]{2,1,0:T(8,128)S(1)}, f32[8,8,64,128]{3,2,1,0:T(8,128)S(1)}, f32[8,8,64,128]{3,2,1,0:T(8,128)S(1)}, f32[8,8,128]{2,1,0:T(8,128)S(1)}, ...) custom-call(s32[256]{0:T(256)} %w_hbm.1, s32[128]{0:T(128)} %n_hbm.1, ...), custom_call_target="tpu_custom_call" | custom-call | tf_op jit(solution)/shard_map/gather/pallas_call | solution.py:319
  19.8 5.1 %invert.1 = (f32[8,64,128]{2,1,0:T(8,128)S(1)}, f32[8,64,128]{2,1,0:T(8,128)S(1)}) custom-call(f32[8,8,64,128]{3,2,1,0:T(8,128)S(1)} %get-tuple-element.16.er_ref, f32[8,8,64,128]{3,2,1,0:T(8,128)S(1)} %get-tuple-element.17.ei_ref, f32[8,8,128]{2,1,0:T(8,128)S(1)} %get-tuple-element.18.ur_ref, f32[8,8,128]{2,1,0:T(8,128)S(1)} %get-tuple-element.19.ui_ref, ...), custom_call_target="tpu_custom_call" | custom-call | tf_op jit(solution)/shard_map/invert/pallas_call | solution.py:430
  24.9 16.7 %leave.1 = f32[16,2,128]{2,1,0:T(2,128)S(1)} custom-call(f32[8,64,128]{2,1,0:T(8,128)S(1)} %get-tuple-element.15.g_ref, f32[8,64,128]{2,1,0:T(8,128)S(1)} %get-tuple-element.23.tr_ref, f32[8,64,128]{2,1,0:T(8,128)S(1)} %get-tuple-element.24.ti_ref), custom_call_target="tpu_custom_call" | custom-call | tf_op jit(solution)/shard_map/leave/pallas_call | solution.py:510
  41.6 0.2 reshape.6
  41.9 0.7 %copy.8 = f32[16,256]{1,0:T(8,128)} copy(f32[16,256]{0,1:T(8,128)S(1)} %bitcast.3) | data formatting | bytes 32768 | tf_op jit(solution)/shard_map/reshape | solution.py:535
  (1 shorter events, 0.0 us)

commit v5 on v4

--- a/solution.py
+++ b/solution.py
@@ -92,7 +92,7 @@
 def gather_kernel(
     w_hbm, n_hbm, h_hbm, s_hbm, g_hbm,
     gall, er_ref, ei_ref, ur_ref, ui_ref, tr_ref, ti_ref, count_ref,
-    w_ref, n_ref, h_ref, hall, sall, wh, wl, hcol, hrow, gcat, gz, zcol, zrow, gh_ref,
+    w_ref, n_ref, h_ref, s_ref, hall, zall, wh, wl, hcol, hrow, gcat, gz, zcol, zrow,
     zs, zr, ps, pr, ss, sr, gs, gr, own,
 ):
     f = lax.axis_index("freq")
@@ -112,8 +112,9 @@
     def along_x(dx):
         return on_freq((x + dx) % XS * LINE + t)
 
-    def paired(one, two):
-        return jnp.where(first, one, swap(two)), jnp.where(first, swap(one), two)
+    def both_parts(value):
+        turned = swap(value)
+        return jnp.concatenate([jnp.where(first, value, turned), jnp.where(first, turned, value)], 1)
 
     def as_right(real, imag):
         def build(r, i):
@@ -132,21 +133,33 @@
     def diagonal_row(value):
         return jnp.sum(jnp.where(eye_mask, value, 0.0), 0, keepdims=True)
 
+    def freq_of(slot, b):
+        return (x + XS - SLOT_DX[slot]) % XS * (PER_FREQ * LINE) + t * PER_FREQ + b
+
+    def share_freq(b):
+        matsubara = (2 * freq_of(0, b) + 1).astype(F32) * (math.pi / (2 * FREQ))
+        zed = jnp.where(eye_mask, jnp.where(first, chem_potential, matsubara), 0.0) - s_ref[b]
+        turned = swap(zed)
+        right = jnp.concatenate([zed, jnp.where(first, -turned, turned)], 0)
+        zall[b, :NORB] = product3(halves(gall[b]), halves(right))
+        zall[b, NORB:] = jnp.broadcast_to(diagonal_row(zed), (8, WIDE))
+
     def prepare_freqs(slot):
-        owner = (x + XS - SLOT_DX[slot]) % XS
         for b in range(PER_FREQ):
             n = slot * PER_FREQ + b
-            freq_id = owner * (PER_FREQ * LINE) + t * PER_FREQ + b
-            count_ref[n : n + 1] = jnp.full((1, WIDE), n_ref[freq_id].astype(F32))
-            matsubara = (2 * freq_id + 1).astype(F32) * (math.pi / (2 * FREQ))
-            shift = jnp.where(first, chem_potential, matsubara)
-            zed = jnp.where(eye_mask, shift, 0.0) - sall[n]
-            real, imag = paired(zed, zed)
-            g_high, g_low = halves(gall[n])
-            gz[n] = product3((g_high, g_low), as_right(real, imag))
-            gcat[n] = jnp.concatenate([g_high, g_low], 1)
-            zcol[n] = jnp.concatenate([diagonal_columns(real), diagonal_columns(imag)], 1)
-            zrow[n : n + 1] = jnp.concatenate([diagonal_row(real), diagonal_row(imag)], 1)
+            count_ref[n : n + 1] = jnp.full((1, WIDE), n_ref[freq_of(slot, b)].astype(F32))
+            product, row = zall[n, :NORB], zall[n, NORB : NORB + 1]
+            gcat[n] = jnp.concatenate(halves(gall[n]), 1)
+            gz[n] = both_parts(product)
+            zrow[n : n + 1] = jnp.concatenate(
+                [jnp.where(first[:1], row, swap(row)), jnp.where(first[:1], swap(row), row)], 1
+            )
+            kept = jnp.where(eye_mask, row, 0.0)
+            real = jnp.sum(jnp.where(first, kept, 0.0), 1, keepdims=True)
+            imag = jnp.sum(jnp.where(first, 0.0, kept), 1, keepdims=True)
+            zcol[n] = jnp.concatenate(
+                [jnp.broadcast_to(part, (NORB, WIDE)) for part in (real, imag, imag * imag)], 1
+            )
 
     def prepare_pair(p):
         one, two = hall[p, 0], hall[p, 1]
@@ -163,17 +176,17 @@
         hrow[p : p + 1] = diagonal_row(real)
 
     first_rows = pl.ds(0, PER_FREQ)
-    own_h, own_s, own_g = hall.at[0, 0], sall.at[first_rows], gall.at[first_rows]
+    own_h, own_z, own_g = hall.at[0, 0], zall.at[first_rows], gall.at[first_rows]
     loads = [
         pltpu.make_async_copy(src, dst, own.at[i])
         for i, (src, dst) in enumerate(
-            ((h_hbm.at[0], h_ref), (g_hbm, own_g), (s_hbm, own_s), (w_hbm, w_ref), (n_hbm, n_ref))
+            ((h_hbm.at[0], h_ref), (g_hbm, own_g), (s_hbm, s_ref), (w_hbm, w_ref), (n_hbm, n_ref))
         )
     ]
     for load in loads:
         load.start()
     await_greetings = greet(
-        [partner] + [along_z(dz) for dz in range(1, ZS)] + [along_x(dx) for dx in range(1, XS)]
+        [along_z(dz) for dz in Z_ORDER] + [along_x(dx) for dx in (2, 1, 3)] + [partner]
     )
     tr_ref[...] = jnp.zeros_like(tr_ref)
     ti_ref[...] = jnp.zeros_like(ti_ref)
@@ -182,6 +195,8 @@
     h = h_ref[...]
     folded = jnp.where(above ^ first, h, swap(h))
     own_h[...] = jnp.where(first[:half], folded[:half], folded[half:])
+    for b in range(PER_FREQ):
+        share_freq(b)
     prepare_freqs(0)
 
     def add_up(i, total):
@@ -201,14 +216,14 @@
     def freq_copies(slot):
         rows = pl.ds(slot * PER_FREQ, PER_FREQ)
         if slot < 3:
-            g_from, s_from = own_g, own_s
-            g_to = s_to = along_x(SLOT_DX[slot])
+            g_from, z_from = own_g, own_z
+            g_to = z_to = along_x(SLOT_DX[slot])
         else:
             g_from, g_to = gall.at[pl.ds(1 * PER_FREQ, PER_FREQ)], along_x(1)
-            s_from, s_to = sall.at[pl.ds(2 * PER_FREQ, PER_FREQ)], along_x(XS - 1)
+            z_from, z_to = zall.at[pl.ds(2 * PER_FREQ, PER_FREQ)], along_x(XS - 1)
         return (
             send(g_from, gall.at[rows], gs.at[slot], gr.at[slot], g_to),
-            send(s_from, sall.at[rows], ss.at[slot], sr.at[slot], s_to),
+            send(z_from, zall.at[rows], ss.at[slot], sr.at[slot], z_to),
         )
 
     started = []
@@ -228,9 +243,7 @@
     def residuals(p, low, high):
         left = gcat[low:high].reshape((high - low) * NORB, 2 * WIDE)
         right = wh[p]
-        gh_ref[: (high - low) * NORB] = dot(left, jnp.concatenate([right, right], 0)) + dot(
-            left[:, :WIDE], wl[p]
-        )
+        gh = dot(left, jnp.concatenate([right, right], 0)) + dot(left[:, :WIDE], wl[p])
         h_diag = hcol[p]
         chip = x * LINE + (z + ZS - p) % ZS * CORES
         w_one = w_ref[(chip + c) * YS + y].astype(F32) * inv_total
@@ -241,11 +254,11 @@
         ur_ref[p, low:high] = d_real * inv
         ui_ref[p, low:high] = -d_imag * inv
         for n in range(low, high):
-            a = gz[n] - gh_ref[(n - low) * NORB : (n - low + 1) * NORB]
+            a = gz[n] - gh[(n - low) * NORB : (n - low + 1) * NORB]
             a_real, a_imag = a[:, :WIDE], a[:, WIDE:]
             d = zcol[n]
-            d_real, d_imag = d[:, :WIDE] - h_diag, d[:, WIDE:]
-            inv = 1.0 / (d_real * d_real + d_imag * d_imag)
+            d_real, d_imag = d[:, :WIDE] - h_diag, d[:, WIDE : 2 * WIDE]
+            inv = 1.0 / (d_real * d_real + d[:, 2 * WIDE :])
             v_real, v_imag = d_real * inv, d_imag * inv
             e_real = eye - (v_real * a_real + v_imag * a_imag)
             e_imag = v_imag * a_real - v_real * a_imag
@@ -269,34 +282,34 @@
         for dz in steps:
             residuals(dz, 0, PER_FREQ)
 
-    near_g, near_s = freq_copies(1), freq_copies(2)
+    near_g, near_z = freq_copies(1), freq_copies(2)
     far = freq_copies(3)
     arrived_pair(0)
     arrived_z(1, 7)
     near_g[0].wait_recv()
     begin(far[0])
-    near_s[1].wait_recv()
+    near_z[1].wait_recv()
     begin(far[1])
     arrived_z(2, 6)
     arrived_pair(1, 7)
-    arrived_z(3, 5)
-    arrived_pair(2, 6)
     near_g[1].wait_recv()
-    near_s[0].wait_recv()
+    near_z[0].wait_recv()
     prepare_freqs(1)
     prepare_freqs(2)
+    arrived_z(3, 5)
+
+    def near_freqs(*pairs):
+        for p in pairs:
+            residuals(p, PER_FREQ, 3 * PER_FREQ)
+
+    near_freqs(0, 1, 7)
     arrived_z(4)
+    arrived_pair(2, 6)
+    near_freqs(2, 6)
     arrived_pair(3, 5)
-
-    def near_freqs(q, carry):
-        residuals(1 + q, PER_FREQ, 3 * PER_FREQ)
-        residuals(ZS - 1 - q, PER_FREQ, 3 * PER_FREQ)
-        return carry
-
-    lax.fori_loop(0, 3, near_freqs, 0)
+    near_freqs(3, 5)
     arrived_pair(4)
-    residuals(0, PER_FREQ, 3 * PER_FREQ)
-    residuals(4, PER_FREQ, 3 * PER_FREQ)
+    near_freqs(4)
     for copy in far:
         copy.wait_recv()
     prepare_freqs(3)
@@ -326,17 +339,17 @@
             pltpu.SMEM((KPTS,), jnp.int32),
             pltpu.SMEM((FREQ,), jnp.int32),
             pltpu.VMEM((NORB, WIDE), F32),
+            pltpu.VMEM((PER_FREQ, NORB, WIDE), F32),
             pltpu.VMEM((ZS, CORES, NORB // 2, WIDE), F32),
-            pltpu.VMEM((N_LOCAL, NORB, WIDE), F32),
+            pltpu.VMEM((N_LOCAL, NORB + 8, WIDE), F32),
             pltpu.VMEM((PAIRS, WIDE, 2 * WIDE), BF),
             pltpu.VMEM((PAIRS, WIDE, 2 * WIDE), BF),
             pltpu.VMEM((PAIRS, NORB, WIDE), F32),
             pltpu.VMEM((PAIRS, WIDE), F32),
             pltpu.VMEM((N_LOCAL, NORB, 2 * WIDE), BF),
             pltpu.VMEM((N_LOCAL, NORB, 2 * WIDE), F32),
-            pltpu.VMEM((N_LOCAL, NORB, 2 * WIDE), F32),
+            pltpu.VMEM((N_LOCAL, NORB, 3 * WIDE), F32),
             pltpu.VMEM((N_LOCAL, 2 * WIDE), F32),
-            pltpu.VMEM((N_LOCAL * NORB, 2 * WIDE), F32),
         ]
         + [dma((ZS,))] * 4
         + [dma((XS,))] * 4
@@ -443,8 +456,9 @@
     y = lax.axis_index("kgrp")
     x, t = f // LINE, f % LINE
     z, c = t // CORES, t % CORES
-    plane = [(dx, dy) for dx in range(XS) for dy in range(YS) if dx or dy]
-    line = [(dz, dc) for dz in range(ZS) for dc in range(CORES) if dz or dc]
+    plane = [(dx, dy) for dx in (2, 1, 3, 0) for dy in (2, 1, 3, 0) if dx or dy]
+    plane.sort(key=lambda step: -min(step[0], XS - step[0]) - min(step[1], YS - step[1]))
+    line = [(dz, dc) for dz in (4, 3, 5, 2, 6, 1, 7, 0) for dc in (1, 0) if dz or dc]
 
     def in_plane(dx, dy):
         return {"freq": (x + dx) % XS * LINE + t, "kgrp": (y + dy) % YS}
@@ -452,7 +466,7 @@
     def place(dz, dc):
         return (z + dz) % ZS * CORES + (c + dc) % CORES
 
-    await_greetings = greet([in_plane(*d) for d in plane] + [on_freq(x * LINE + place(*d)) for d in line])
+    await_greetings = greet([q for d, e in zip(plane, line) for q in (in_plane(*d), on_freq(x * LINE + place(*e)))])
     lanes, first, _ = lane_masks()
     quarter = lanes % NORB // (NORB // YS)
     for n_high in range(2):
@@ -483,7 +497,7 @@
         copy.start()
         started.append(copy)
     total = o_ref[x, y]
-    for dx, dy in plane:
+    for dx, dy in reversed(plane):
         slot = dx * YS + dy
         send(o_ref.at[x, y], landed.at[slot], as_.at[slot], ar.at[slot], in_plane(dx, dy)).wait_recv()
         total = total + landed[slot]
@@ -497,7 +511,7 @@
         copy.start()
         started.append(copy)
     q_ref[pl.ds(t, 1)] = rows_ref[pl.ds(t, 1)]
-    for dz, dc in line:
+    for dz, dc in reversed(line):
         slot = dz * CORES + dc
         source = (z + ZS - dz) % ZS * CORES + (c + CORES - dc) % CORES
         send(rows_ref.at[source], q_ref.at[source], bs.at[slot], br.at[slot], on_freq(x * LINE + place(dz, dc))).wait_recv()

time: 42 us -> 39.7 us (0.945); the launches traced: 42.6 us -> 39.6 us
  Pallas kernels: 41.6 us -> 38.6 us
    pallas_call x1, Pallas kernels: 16.7 us -> 15.6 us  [leave(): pl.pallas_call(exit_kernel, name='leave', out_shape=jax.ShapeDtypeStruct(...]
    pallas_call x1, Pallas kernels: 19.8 us -> 18.7 us  [gather(): pl.pallas_call(gather_kernel, name='gather', out_shape=(totals, powers, p...]
    pallas_call x1, Pallas kernels: 5.07 us -> 4.34 us  [invert(): pl.pallas_call(power_kernel, name='invert', out_shape=(totals, totals), i...]
where the time goes in v5:
time: 39.7 us; the launch traced here: 39.6 us
  Pallas kernels  38.6 us (97%)
  local copies, waits for them, and re-layouts  0.95 us (2%)
    pallas_call x1, Pallas kernels, gather(): pl.pallas_call(gather_kernel, name='gather', out_shape=(totals, powers, p...  18.7 us
    pallas_call x1, Pallas kernels, leave(): pl.pallas_call(exit_kernel, name='leave', out_shape=jax.ShapeDtypeStruct(...  15.6 us
    pallas_call x1, Pallas kernels, invert(): pl.pallas_call(power_kernel, name='invert', out_shape=(totals, totals), i...  4.34 us

profile of v5, /device:TPU:1, one launch (start us, length us, event | category | flops | bytes accessed | tf_op | source)
XLA Modules:
  0.0 39.6 jit_solution(2022581315539726407)
XLA Ops:
  0.0 18.7 %gather.1 = (f32[8,64,128]{2,1,0:T(8,128)S(1)}, f32[8,8,64,128]{3,2,1,0:T(8,128)S(1)}, f32[8,8,64,128]{3,2,1,0:T(8,128)S(1)}, f32[8,8,128]{2,1,0:T(8,128)S(1)}, ...) custom-call(s32[256]{0:T(256)} %w_hbm.1, s32[128]{0:T(128)} %n_hbm.1, ...), custom_call_target="tpu_custom_call" | custom-call | tf_op jit(solution)/shard_map/gather/pallas_call | solution.py:332
  18.7 4.3 %invert.1 = (f32[8,64,128]{2,1,0:T(8,128)S(1)}, f32[8,64,128]{2,1,0:T(8,128)S(1)}) custom-call(f32[8,8,64,128]{3,2,1,0:T(8,128)S(1)} %get-tuple-element.16.er_ref, f32[8,8,64,128]{3,2,1,0:T(8,128)S(1)} %get-tuple-element.17.ei_ref, f32[8,8,128]{2,1,0:T(8,128)S(1)} %get-tuple-element.18.ur_ref, f32[8,8,128]{2,1,0:T(8,128)S(1)} %get-tuple-element.19.ui_ref, ...), custom_call_target="tpu_custom_call" | custom-call | tf_op jit(solution)/shard_map/invert/pallas_call | solution.py:443
  23.0 15.6 %leave.1 = f32[16,2,128]{2,1,0:T(2,128)S(1)} custom-call(f32[8,64,128]{2,1,0:T(8,128)S(1)} %get-tuple-element.15.g_ref, f32[8,64,128]{2,1,0:T(8,128)S(1)} %get-tuple-element.23.tr_ref, f32[8,64,128]{2,1,0:T(8,128)S(1)} %get-tuple-element.24.ti_ref), custom_call_target="tpu_custom_call" | custom-call | tf_op jit(solution)/shard_map/leave/pallas_call | solution.py:524
  38.6 0.2 reshape.6
  38.9 0.7 %copy.8 = f32[16,256]{1,0:T(8,128)} copy(f32[16,256]{0,1:T(8,128)S(1)} %bitcast.3) | data formatting | bytes 32768 | tf_op jit(solution)/shard_map/reshape | solution.py:549
  (1 shorter events, 0.0 us)

commit v6 on v5

--- a/solution.py
+++ b/solution.py
@@ -91,7 +91,7 @@
 
 def gather_kernel(
     w_hbm, n_hbm, h_hbm, s_hbm, g_hbm,
-    gall, er_ref, ei_ref, ur_ref, ui_ref, tr_ref, ti_ref, count_ref,
+    gall, er_ref, ei_ref, ur_ref, ui_ref, count_ref,
     w_ref, n_ref, h_ref, s_ref, hall, zall, wh, wl, hcol, hrow, gcat, gz, zcol, zrow,
     zs, zr, ps, pr, ss, sr, gs, gr, own,
 ):
@@ -188,8 +188,6 @@
     await_greetings = greet(
         [along_z(dz) for dz in Z_ORDER] + [along_x(dx) for dx in (2, 1, 3)] + [partner]
     )
-    tr_ref[...] = jnp.zeros_like(tr_ref)
-    ti_ref[...] = jnp.zeros_like(ti_ref)
     for load in loads:
         load.wait()
     h = h_ref[...]
@@ -264,10 +262,6 @@
             e_imag = v_imag * a_real - v_real * a_imag
             er_ref[n, p] = e_real
             ei_ref[n, p] = e_imag
-            u_real, u_imag = ur_ref[p, n : n + 1], ui_ref[p, n : n + 1]
-            q_real = eye + e_real
-            tr_ref[n] += q_real * u_real - e_imag * u_imag
-            ti_ref[n] += q_real * u_imag + e_imag * u_real
 
     def arrived_z(*steps):
         for dz in steps:
@@ -332,9 +326,9 @@
     return pl.pallas_call(
         gather_kernel,
         name="gather",
-        out_shape=(totals, powers, powers, scales, scales, totals, totals, counted),
+        out_shape=(totals, powers, powers, scales, scales, counted),
         in_specs=[hbm()] * 5,
-        out_specs=(vmem(),) * 8,
+        out_specs=(vmem(),) * 6,
         scratch_shapes=[
             pltpu.SMEM((KPTS,), jnp.int32),
             pltpu.SMEM((FREQ,), jnp.int32),
@@ -361,7 +355,7 @@
 
 
 def power_kernel(
-    er_ref, ei_ref, ur_ref, ui_ref, t1r_ref, t1i_ref, count_ref, tr_ref, ti_ref, sr_ref, si_ref, qr_ref, qi_ref, steps_ref
+    er_ref, ei_ref, ur_ref, ui_ref, count_ref, tr_ref, ti_ref, sr_ref, si_ref, qr_ref, qi_ref, steps_ref
 ):
     _, first, eye_mask = lane_masks()
     eye = eye_mask.astype(F32)
@@ -396,12 +390,12 @@
         for p in range(PAIRS):
             e_real, e_imag = er_ref[n, p], ei_ref[n, p]
             sr_ref[p], si_ref[p] = combine(product3(left_rows(e_real, e_imag), right_blocks(e_real, e_imag)))
-        total = t1r_ref[n], t1i_ref[n]
+        total = None
         for p in range(PAIRS):
-            left = left_rows(eye + er_ref[n, p], ei_ref[n, p])
-            real, imag = combine(product3(left, right_blocks(sr_ref[p], si_ref[p])))
-            real, imag = weighted(n, p, real, imag)
-            total = total[0] + real, total[1] + imag
+            q_real, q_imag = eye + er_ref[n, p], ei_ref[n, p]
+            real, imag = combine(product3(left_rows(q_real, q_imag), right_blocks(sr_ref[p], si_ref[p])))
+            real, imag = weighted(n, p, q_real + real, q_imag + imag)
+            total = (real, imag) if total is None else (total[0] + real, total[1] + imag)
         tr_ref[n], ti_ref[n] = total
 
     def three_steps(n):
@@ -425,8 +419,8 @@
 
     for n in range(N_LOCAL):
         steps_ref[n] = jnp.max(count_ref[n : n + 1])
-    tr_ref[...] = t1r_ref[...]
-    ti_ref[...] = t1i_ref[...]
+    tr_ref[...] = jnp.zeros_like(tr_ref)
+    ti_ref[...] = jnp.zeros_like(ti_ref)
 
     def one_freq(n, carry):
         steps = steps_ref[n]
@@ -444,14 +438,16 @@
         power_kernel,
         name="invert",
         out_shape=(totals, totals),
-        in_specs=[vmem()] * 7,
+        in_specs=[vmem()] * 5,
         out_specs=(vmem(),) * 2,
         scratch_shapes=[slots] * 4 + [pltpu.SMEM((N_LOCAL,), F32)],
         compiler_params=pltpu.CompilerParams(vmem_limit_bytes=16 << 20),
     )(*gathered)
 
 
-def exit_kernel(g_ref, tr_ref, ti_ref, q_ref, o_ref, landed, rows_ref, as_, ar, bs, br):
+def exit_kernel(
+    g_ref, er_ref, ei_ref, ur_ref, ui_ref, count_ref, tr_ref, ti_ref, q_ref, o_ref, t_ref, landed, rows_ref, as_, ar, bs, br
+):
     f = lax.axis_index("freq")
     y = lax.axis_index("kgrp")
     x, t = f // LINE, f % LINE
@@ -467,8 +463,23 @@
         return (z + dz) % ZS * CORES + (c + dc) % CORES
 
     await_greetings = greet([q for d, e in zip(plane, line) for q in (in_plane(*d), on_freq(x * LINE + place(*e)))])
-    lanes, first, _ = lane_masks()
+    lanes, first, eye_mask = lane_masks()
+    eye = eye_mask.astype(F32)
     quarter = lanes % NORB // (NORB // YS)
+
+    def one_step(n, carry):
+        t_real = t_imag = jnp.zeros((NORB, WIDE), F32)
+        for p in range(PAIRS):
+            q_real, q_imag = eye + er_ref[n, p], ei_ref[n, p]
+            u_real, u_imag = ur_ref[p, pl.ds(n, 1)], ui_ref[p, pl.ds(n, 1)]
+            t_real = t_real + (q_real * u_real - q_imag * u_imag)
+            t_imag = t_imag + (q_real * u_imag + q_imag * u_real)
+        single = count_ref[pl.ds(n, 1)] < 1.5
+        t_real, t_imag = jnp.where(single, t_real, tr_ref[n]), jnp.where(single, t_imag, ti_ref[n])
+        t_ref[n] = jnp.where(first, t_real + swap(t_real), t_imag + swap(t_imag))
+        return carry
+
+    lax.fori_loop(0, N_LOCAL, one_step, 0)
     for n_high in range(2):
         mixed = [None] * YS
         for n_low in range(4):
@@ -476,10 +487,9 @@
             n = (dx + dx // 2 * (5 - 2 * dx)) * PER_FREQ + n_low % 2
             g = g_ref[n]
             turned = jnp.where(first, -swap(g), swap(g))
-            r_high, r_low = halves(jnp.concatenate([g, g, turned, turned], 0))
-            l_high, l_low = halves(jnp.concatenate([tr_ref[n], ti_ref[n]], 1))
-            both = dot(l_high, jnp.concatenate([r_high, r_low], 1))
-            value = both[:, :WIDE] + both[:, WIDE:] + dot(l_low, r_high)
+            right = jnp.concatenate(halves(jnp.concatenate([g, turned], 0)), 1)
+            both = dot(jnp.concatenate(halves(t_ref[n]), 1), jnp.concatenate([right, right], 0))
+            value = both[:, :WIDE] + both[:, WIDE:]
             for to_y in range(YS):
                 shift = (n_low - to_y) * (NORB // YS) % WIDE
                 moved = pltpu.roll(value, shift, 1) if shift else value
@@ -525,10 +535,11 @@
         exit_kernel,
         name="leave",
         out_shape=jax.ShapeDtypeStruct((LINE, 2, WIDE), F32),
-        in_specs=[vmem()] * 3,
+        in_specs=[vmem()] * 8,
         out_specs=vmem(),
         scratch_shapes=[
             pltpu.VMEM((XS, YS, 2, LINE, WIDE), F32),
+            pltpu.VMEM((N_LOCAL, NORB, WIDE), F32),
             pltpu.VMEM((XS * YS, 2, LINE, WIDE), F32),
             pltpu.VMEM((LINE, 2, WIDE), F32),
             dma((XS * YS,)),
@@ -544,7 +555,7 @@
 
 def per_device(hamiltonian, self_energy, guess_factor, weights, counts):
     g_all, *gathered = gather(weights, counts, hamiltonian, self_energy, guess_factor)
-    arrived = leave(g_all, *invert(*gathered))
+    arrived = leave(g_all, *gathered, *invert(*gathered))
     pieces = arrived.reshape(LINE, 2, 2, 2, 2, NORB // YS)
     return pieces.transpose(5, 2, 1, 3, 0, 4).reshape(NORB // YS, 2 * FREQ)
 

time: 39.7 us -> 40.4 us (1.018)
  Pallas kernels: 38.6 us -> 39.3 us
    pallas_call x1, Pallas kernels: 15.6 us -> 18.1 us  [leave(): pl.pallas_call(exit_kernel, name='leave', out_shape=jax.ShapeDtypeStruct(...]
    pallas_call x1, Pallas kernels: 4.34 us -> 2.86 us  [invert(): pl.pallas_call(power_kernel, name='invert', out_shape=(totals, totals), i...]
where the time goes in v6:
time: 40.4 us; the launch traced here: 40.3 us
  Pallas kernels  39.3 us (97%)
  local copies, waits for them, and re-layouts  0.95 us (2%)
    pallas_call x1, Pallas kernels, gather(): pl.pallas_call(gather_kernel, name='gather', out_shape=(totals, powers, p...  18.3 us
    pallas_call x1, Pallas kernels, leave(): pl.pallas_call(exit_kernel, name='leave', out_shape=jax.ShapeDtypeStruct(...  18.1 us
    pallas_call x1, Pallas kernels, invert(): pl.pallas_call(power_kernel, name='invert', out_shape=(totals, totals), i...  2.86 us

profile of v6, /device:TPU:1, one launch (start us, length us, event | category | flops | bytes accessed | tf_op | source)
XLA Modules:
  0.0 40.3 jit_solution(15454704443086199884)
XLA Ops:
  0.0 18.3 %gather.1 = (f32[8,64,128]{2,1,0:T(8,128)S(1)}, f32[8,8,64,128]{3,2,1,0:T(8,128)S(1)}, f32[8,8,64,128]{3,2,1,0:T(8,128)S(1)}, f32[8,8,128]{2,1,0:T(8,128)S(1)}, ...) custom-call(s32[256]{0:T(256)} %w_hbm.1, s32[128]{0:T(128)} %n_hbm.1, f32[1,64,128]{2,1,0:T(8,128)} %h_hbm.1, ...), custom_call_target="tpu_custom_call" | custom-call | tf_op jit(solution)/shard_map/gather/pallas_call | solution.py:326
  18.3 2.9 %invert.1 = (f32[8,64,128]{2,1,0:T(8,128)S(1)}, f32[8,64,128]{2,1,0:T(8,128)S(1)}) custom-call(f32[8,8,64,128]{3,2,1,0:T(8,128)S(1)} %get-tuple-element.14.er_ref, f32[8,8,64,128]{3,2,1,0:T(8,128)S(1)} %get-tuple-element.15.ei_ref, f32[8,8,128]{2,1,0:T(8,128)S(1)} %get-tuple-element.16.ur_ref, f32[8,8,128]{2,1,0:T(8,128)S(1)} %get-tuple-element.17.ui_ref, ...), custom_call_target="tpu_custom_call" | custom-call | tf_op jit(solution)/shard_map/invert/pallas_call | solution.py:437
  21.2 18.1 %leave.1 = f32[16,2,128]{2,1,0:T(2,128)S(1)} custom-call(f32[8,64,128]{2,1,0:T(8,128)S(1)} %get-tuple-element.13.g_ref, f32[8,8,64,128]{3,2,1,0:T(8,128)S(1)} %get-tuple-element.14.er_ref, f32[8,8,64,128]{3,2,1,0:T(8,128)S(1)} %get-tuple-element.15.ei_ref, f32[8,8,128]{2,1,0:T(8,128)S(1)} %get-tuple-element.16.ur_ref, ...), custom_call_target="tpu_custom_call" | custom-call | tf_op jit(solution)/shard_map/leave/pallas_call | solution.py:534
  39.3 0.2 reshape.6
  39.6 0.7 %copy.8 = f32[16,256]{1,0:T(8,128)} copy(f32[16,256]{0,1:T(8,128)S(1)} %bitcast.3) | data formatting | bytes 32768 | tf_op jit(solution)/shard_map/reshape | solution.py:560
  (1 shorter events, 0.0 us)

commit v7 on v6

--- a/solution.py
+++ b/solution.py
@@ -87,6 +87,32 @@
     rows = lax.broadcasted_iota(jnp.int32, (NORB, WIDE), 0)
     lanes = lax.broadcasted_iota(jnp.int32, (NORB, WIDE), 1)
     return lanes, lanes < NORB, rows == lanes % NORB
+
+
+def right_blocks(real, imag):
+    first = lane_masks()[1].astype(F32)
+    first_bf, second_bf = first.astype(BF), (1.0 - first).astype(BF)
+
+    def build(r, i):
+        return jnp.concatenate(
+            [
+                jnp.concatenate([r * first_bf, i * first_bf], 1),
+                jnp.concatenate([r * second_bf, i * second_bf], 1),
+            ],
+            0,
+        )
+
+    r_high, r_low = halves(real)
+    i_high, i_low = halves(imag)
+    return build(r_high, i_high), build(r_low, i_low)
+
+
+def left_rows(real, imag):
+    return halves(jnp.concatenate([real, imag], 0))
+
+
+def combine(out):
+    return out[:NORB, :WIDE] - out[NORB:, WIDE:], out[:NORB, WIDE:] + out[NORB:, :WIDE]
 
 
 def gather_kernel(
@@ -302,17 +328,15 @@
     near_freqs(2, 6)
     arrived_pair(3, 5)
     near_freqs(3, 5)
-    arrived_pair(4)
-    near_freqs(4)
     for copy in far:
         copy.wait_recv()
     prepare_freqs(3)
 
-    def far_freqs(p, carry):
+    for p in (0, 1, 7, 2, 6, 3, 5):
         residuals(p, 3 * PER_FREQ, N_LOCAL)
-        return carry
-
-    lax.fori_loop(0, PAIRS, far_freqs, 0, unroll=4)
+    partner_copy(4).wait_recv()
+    prepare_pair(4)
+    residuals(4, 0, N_LOCAL)
     for copy in started:
         copy.wait_send()
 
@@ -354,76 +378,37 @@
     )(*(pltpu.with_memory_space_constraint(value, pltpu.HBM) for value in values))
 
 
-def power_kernel(
-    er_ref, ei_ref, ur_ref, ui_ref, count_ref, tr_ref, ti_ref, sr_ref, si_ref, qr_ref, qi_ref, steps_ref
-):
-    _, first, eye_mask = lane_masks()
-    eye = eye_mask.astype(F32)
-    first_bf = first.astype(F32).astype(BF)
-    second_bf = (1.0 - first.astype(F32)).astype(BF)
-
-    def right_blocks(real, imag):
-        def build(r, i):
-            return jnp.concatenate(
-                [
-                    jnp.concatenate([r * first_bf, i * first_bf], 1),
-                    jnp.concatenate([r * second_bf, i * second_bf], 1),
-                ],
-                0,
-            )
-
-        r_high, r_low = halves(real)
-        i_high, i_low = halves(imag)
-        return build(r_high, i_high), build(r_low, i_low)
-
-    def left_rows(real, imag):
-        return halves(jnp.concatenate([real, imag], 0))
-
-    def combine(out):
-        return out[:NORB, :WIDE] - out[NORB:, WIDE:], out[:NORB, WIDE:] + out[NORB:, :WIDE]
-
-    def weighted(n, p, real, imag):
-        u_real, u_imag = ur_ref[p, pl.ds(n, 1)], ui_ref[p, pl.ds(n, 1)]
-        return real * u_real - imag * u_imag, real * u_imag + imag * u_real
-
-    def two_steps(n):
+def power_kernel(e_in_real, e_in_imag, count_ref, er_ref, ei_ref, br_ref, bi_ref, sr_ref, si_ref, steps_ref):
+    eye = lane_masks()[2].astype(F32)
+
+    def one_step(n):
+        for p in range(PAIRS):
+            br_ref[n, p] = bi_ref[n, p] = jnp.zeros((NORB, WIDE), F32)
+
+    def squares(n, real_ref, imag_ref):
         for p in range(PAIRS):
             e_real, e_imag = er_ref[n, p], ei_ref[n, p]
-            sr_ref[p], si_ref[p] = combine(product3(left_rows(e_real, e_imag), right_blocks(e_real, e_imag)))
-        total = None
-        for p in range(PAIRS):
-            q_real, q_imag = eye + er_ref[n, p], ei_ref[n, p]
-            real, imag = combine(product3(left_rows(q_real, q_imag), right_blocks(sr_ref[p], si_ref[p])))
-            real, imag = weighted(n, p, q_real + real, q_imag + imag)
-            total = (real, imag) if total is None else (total[0] + real, total[1] + imag)
-        tr_ref[n], ti_ref[n] = total
+            real_ref[p], imag_ref[p] = combine(product3(left_rows(e_real, e_imag), right_blocks(e_real, e_imag)))
+
+    def two_steps(n):
+        squares(n, br_ref.at[n], bi_ref.at[n])
 
     def three_steps(n):
-        for p in range(PAIRS):
-            e_real, e_imag = er_ref[n, p], ei_ref[n, p]
-            sr_ref[p], si_ref[p] = combine(product3(left_rows(e_real, e_imag), right_blocks(e_real, e_imag)))
+        squares(n, sr_ref, si_ref)
         for p in range(PAIRS):
             e_real, e_imag = er_ref[n, p], ei_ref[n, p]
             s_real, s_imag = sr_ref[p], si_ref[p]
             right = right_blocks(s_real, s_imag)
             real, imag = combine(product3(left_rows(eye + e_real, e_imag), right))
-            qr_ref[p], qi_ref[p] = eye + e_real + real, e_imag + imag
-            sr_ref[p], si_ref[p] = combine(product3(left_rows(s_real, s_imag), right))
-        total = None
-        for p in range(PAIRS):
-            q_real, q_imag = qr_ref[p], qi_ref[p]
-            real, imag = combine(product3(left_rows(q_real, q_imag), right_blocks(sr_ref[p], si_ref[p])))
-            real, imag = weighted(n, p, q_real + real, q_imag + imag)
-            total = (real, imag) if total is None else (total[0] + real, total[1] + imag)
-        tr_ref[n], ti_ref[n] = total
+            er_ref[n, p], ei_ref[n, p] = e_real + real, e_imag + imag
+            br_ref[n, p], bi_ref[n, p] = combine(product3(left_rows(s_real, s_imag), right))
 
     for n in range(N_LOCAL):
         steps_ref[n] = jnp.max(count_ref[n : n + 1])
-    tr_ref[...] = jnp.zeros_like(tr_ref)
-    ti_ref[...] = jnp.zeros_like(ti_ref)
 
     def one_freq(n, carry):
         steps = steps_ref[n]
+        pl.when(steps < 1.5)(functools.partial(one_step, n))
         pl.when((steps > 1.5) & (steps < 2.5))(functools.partial(two_steps, n))
         pl.when(steps > 2.5)(functools.partial(three_steps, n))
         return carry
@@ -431,22 +416,23 @@
     lax.fori_loop(0, N_LOCAL, one_freq, 0)
 
 
-def invert(*gathered):
+def invert(*residuals_and_counts):
     slots = pltpu.VMEM((PAIRS, NORB, WIDE), F32)
-    totals = jax.ShapeDtypeStruct((N_LOCAL, NORB, WIDE), F32)
+    powers = jax.ShapeDtypeStruct((N_LOCAL, PAIRS, NORB, WIDE), F32)
     return pl.pallas_call(
         power_kernel,
         name="invert",
-        out_shape=(totals, totals),
-        in_specs=[vmem()] * 5,
-        out_specs=(vmem(),) * 2,
-        scratch_shapes=[slots] * 4 + [pltpu.SMEM((N_LOCAL,), F32)],
-        compiler_params=pltpu.CompilerParams(vmem_limit_bytes=16 << 20),
-    )(*gathered)
+        out_shape=(powers,) * 4,
+        in_specs=[vmem()] * 3,
+        out_specs=(vmem(),) * 4,
+        input_output_aliases={0: 0, 1: 1},
+        scratch_shapes=[slots] * 2 + [pltpu.SMEM((N_LOCAL,), F32)],
+        compiler_params=pltpu.CompilerParams(vmem_limit_bytes=24 << 20),
+    )(*residuals_and_counts)
 
 
 def exit_kernel(
-    g_ref, er_ref, ei_ref, ur_ref, ui_ref, count_ref, tr_ref, ti_ref, q_ref, o_ref, t_ref, landed, rows_ref, as_, ar, bs, br
+    g_ref, ur_ref, ui_ref, er_ref, ei_ref, br_ref, bi_ref, q_ref, o_ref, t_ref, landed, rows_ref, as_, ar, bs, br
 ):
     f = lax.axis_index("freq")
     y = lax.axis_index("kgrp")
@@ -467,19 +453,20 @@
     eye = eye_mask.astype(F32)
     quarter = lanes % NORB // (NORB // YS)
 
-    def one_step(n, carry):
+    def last_product(n, carry):
         t_real = t_imag = jnp.zeros((NORB, WIDE), F32)
         for p in range(PAIRS):
             q_real, q_imag = eye + er_ref[n, p], ei_ref[n, p]
+            right = right_blocks(br_ref[n, p], bi_ref[n, p])
+            real, imag = combine(product3(left_rows(q_real, q_imag), right))
+            q_real, q_imag = q_real + real, q_imag + imag
             u_real, u_imag = ur_ref[p, pl.ds(n, 1)], ui_ref[p, pl.ds(n, 1)]
             t_real = t_real + (q_real * u_real - q_imag * u_imag)
             t_imag = t_imag + (q_real * u_imag + q_imag * u_real)
-        single = count_ref[pl.ds(n, 1)] < 1.5
-        t_real, t_imag = jnp.where(single, t_real, tr_ref[n]), jnp.where(single, t_imag, ti_ref[n])
         t_ref[n] = jnp.where(first, t_real + swap(t_real), t_imag + swap(t_imag))
         return carry
 
-    lax.fori_loop(0, N_LOCAL, one_step, 0)
+    lax.fori_loop(0, N_LOCAL, last_product, 0, unroll=2)
     for n_high in range(2):
         mixed = [None] * YS
         for n_low in range(4):
@@ -535,7 +522,7 @@
         exit_kernel,
         name="leave",
         out_shape=jax.ShapeDtypeStruct((LINE, 2, WIDE), F32),
-        in_specs=[vmem()] * 8,
+        in_specs=[vmem()] * 7,
         out_specs=vmem(),
         scratch_shapes=[
             pltpu.VMEM((XS, YS, 2, LINE, WIDE), F32),
@@ -548,14 +535,16 @@
             dma((LINE,)),
         ],
         compiler_params=pltpu.CompilerParams(
-            collective_id=1, has_side_effects=True, vmem_limit_bytes=8 << 20
+            collective_id=1, has_side_effects=True, vmem_limit_bytes=16 << 20
         ),
     )(*parts)
 
 
 def per_device(hamiltonian, self_energy, guess_factor, weights, counts):
-    g_all, *gathered = gather(weights, counts, hamiltonian, self_energy, guess_factor)
-    arrived = leave(g_all, *gathered, *invert(*gathered))
+    g_all, e_real, e_imag, u_real, u_imag, steps = gather(
+        weights, counts, hamiltonian, self_energy, guess_factor
+    )
+    arrived = leave(g_all, u_real, u_imag, *invert(e_real, e_imag, steps))
     pieces = arrived.reshape(LINE, 2, 2, 2, 2, NORB // YS)
     return pieces.transpose(5, 2, 1, 3, 0, 4).reshape(NORB // YS, 2 * FREQ)
 

time: 40.4 us -> 39 us (0.965)
  Pallas kernels: 39.3 us -> 37.9 us
    pallas_call x1, Pallas kernels: 18.1 us -> 16.9 us  [leave(): pl.pallas_call(exit_kernel, name='leave', out_shape=jax.ShapeDtypeStruct(...]
where the time goes in v7:
time: 39 us; the launch traced here: 38.9 us
  Pallas kernels  37.9 us (97%)
  local copies, waits for them, and re-layouts  0.95 us (2%)
    pallas_call x1, Pallas kernels, gather(): pl.pallas_call(gather_kernel, name='gather', out_shape=(totals, powers, p...  18 us
    pallas_call x1, Pallas kernels, leave(): pl.pallas_call(exit_kernel, name='leave', out_shape=jax.ShapeDtypeStruct(...  16.9 us
    pallas_call x1, Pallas kernels, invert(): pl.pallas_call(power_kernel, name='invert', out_shape=(powers,) * 4, in_s...  2.89 us

profile of v7, /device:TPU:1, one launch (start us, length us, event | category | flops | bytes accessed | tf_op | source)
XLA Modules:
  0.0 38.9 jit_solution(288083357428078922)
XLA Ops:
  0.0 18.0 %gather.1 = (f32[8,64,128]{2,1,0:T(8,128)S(1)}, f32[8,8,64,128]{3,2,1,0:T(8,128)S(1)}, f32[8,8,64,128]{3,2,1,0:T(8,128)S(1)}, f32[8,8,128]{2,1,0:T(8,128)S(1)}, ...) custom-call(s32[256]{0:T(256)} %w_hbm.1, s32[128]{0:T(128)} %n_hbm.1, f32[1,64,128]{2,1,0:T(8,128)} %h_hbm.1, ...), custom_call_target="tpu_custom_call" | custom-call | tf_op jit(solution)/shard_map/gather/pallas_call | solution.py:350
  18.0 2.9 %invert.1 = (f32[8,8,64,128]{3,2,1,0:T(8,128)S(1)}, f32[8,8,64,128]{3,2,1,0:T(8,128)S(1)}, f32[8,8,64,128]{3,2,1,0:T(8,128)S(1)}, f32[8,8,64,128]{3,2,1,0:T(8,128)S(1)}) custom-call(f32[8,8,64,128]{3,2,1,0:T(8,128)S(1)} %get-tuple-element.18.e_in_real, ...), custom_call_target="tpu_custom_call", output_to_operand_aliasing={{0}: (0, {}), {1}: (1, {})} | custom-call | tf_op jit(solution)/shard_map/invert/pallas_call | solution.py:422
  20.9 16.9 %leave.1 = f32[16,2,128]{2,1,0:T(2,128)S(1)} custom-call(f32[8,64,128]{2,1,0:T(8,128)S(1)} %get-tuple-element.15.g_ref, f32[8,8,128]{2,1,0:T(8,128)S(1)} %get-tuple-element.16.ur_ref, f32[8,8,128]{2,1,0:T(8,128)S(1)} %get-tuple-element.17.ui_ref, f32[8,8,64,128]{3,2,1,0:T(8,128)S(1)} %get-tuple-element.21.er_ref, ...), custom_call_target="tpu_custom_call" | custom-call | tf_op jit(solution)/shard_map/leave/pallas_call | solution.py:521
  37.9 0.2 reshape.6
  38.2 0.7 %copy.10 = f32[16,256]{1,0:T(8,128)} copy(f32[16,256]{0,1:T(8,128)S(1)} %bitcast.3) | data formatting | bytes 32768 | tf_op jit(solution)/shard_map/reshape | solution.py:549
  (1 shorter events, 0.0 us)

commit v8 on v7

--- a/solution.py
+++ b/solution.py
@@ -294,49 +294,51 @@
             z_copy(dz).wait_recv()
             begin(partner_copy(dz))
 
-    def arrived_pair(*steps):
+    def await_pairs(*steps):
         for dz in steps:
             partner_copy(dz).wait_recv()
-        for dz in steps:
-            prepare_pair(dz)
-        for dz in steps:
-            residuals(dz, 0, PER_FREQ)
+
+    def all_residuals(pairs, low, high):
+        for p in pairs:
+            residuals(p, low, high)
+
+    def prepare_pairs(*pairs):
+        for p in pairs:
+            prepare_pair(p)
 
     near_g, near_z = freq_copies(1), freq_copies(2)
     far = freq_copies(3)
-    arrived_pair(0)
+    await_pairs(0)
+    prepare_pairs(0)
+    all_residuals((0,), 0, 2)
     arrived_z(1, 7)
     near_g[0].wait_recv()
     begin(far[0])
     near_z[1].wait_recv()
     begin(far[1])
     arrived_z(2, 6)
-    arrived_pair(1, 7)
+    await_pairs(1, 7)
+    prepare_pairs(1, 7)
+    all_residuals((1, 7), 0, 2)
     near_g[1].wait_recv()
     near_z[0].wait_recv()
+    arrived_z(3, 5)
+    await_pairs(2, 6)
     prepare_freqs(1)
     prepare_freqs(2)
-    arrived_z(3, 5)
-
-    def near_freqs(*pairs):
-        for p in pairs:
-            residuals(p, PER_FREQ, 3 * PER_FREQ)
-
-    near_freqs(0, 1, 7)
+    prepare_pairs(2, 6)
+    all_residuals((0, 1, 7), 2, 6)
     arrived_z(4)
-    arrived_pair(2, 6)
-    near_freqs(2, 6)
-    arrived_pair(3, 5)
-    near_freqs(3, 5)
+    await_pairs(3, 5)
+    prepare_pairs(3, 5)
+    all_residuals((2, 6, 3, 5), 0, 6)
     for copy in far:
         copy.wait_recv()
+    await_pairs(4)
     prepare_freqs(3)
-
-    for p in (0, 1, 7, 2, 6, 3, 5):
-        residuals(p, 3 * PER_FREQ, N_LOCAL)
-    partner_copy(4).wait_recv()
-    prepare_pair(4)
-    residuals(4, 0, N_LOCAL)
+    prepare_pairs(4)
+    all_residuals((4,), 0, 6)
+    all_residuals((0, 1, 7, 2, 6, 3, 5, 4), 6, 8)
     for copy in started:
         copy.wait_send()
 
@@ -466,7 +468,7 @@
         t_ref[n] = jnp.where(first, t_real + swap(t_real), t_imag + swap(t_imag))
         return carry
 
-    lax.fori_loop(0, N_LOCAL, last_product, 0, unroll=2)
+    lax.fori_loop(0, N_LOCAL, last_product, 0, unroll=4)
     for n_high in range(2):
         mixed = [None] * YS
         for n_low in range(4):

time: 39 us -> 38.3 us (0.982)
  Pallas kernels: 37.9 us -> 37.4 us
    pallas_call x1, Pallas kernels: 16.9 us -> 16.4 us  [leave(): pl.pallas_call(exit_kernel, name='leave', out_shape=jax.ShapeDtypeStruct(...]
    pallas_call x1, Pallas kernels: 2.89 us -> 3.29 us  [invert(): pl.pallas_call(power_kernel, name='invert', out_shape=(powers,) * 4, in_s...]
where the time goes in v8:
time: 38.3 us; the launch traced here: 38.4 us
  Pallas kernels  37.4 us (98%)
  local copies, waits for them, and re-layouts  0.95 us (2%)
    pallas_call x1, Pallas kernels, gather(): pl.pallas_call(gather_kernel, name='gather', out_shape=(totals, powers, p...  17.7 us
    pallas_call x1, Pallas kernels, leave(): pl.pallas_call(exit_kernel, name='leave', out_shape=jax.ShapeDtypeStruct(...  16.4 us
    pallas_call x1, Pallas kernels, invert(): pl.pallas_call(power_kernel, name='invert', out_shape=(powers,) * 4, in_s...  3.29 us

profile of v8, /device:TPU:1, one launch (start us, length us, event | category | flops | bytes accessed | tf_op | source)
XLA Modules:
  0.0 38.4 jit_solution(4222171220427797084)
XLA Ops:
  0.0 17.7 %gather.1 = (f32[8,64,128]{2,1,0:T(8,128)S(1)}, f32[8,8,64,128]{3,2,1,0:T(8,128)S(1)}, f32[8,8,64,128]{3,2,1,0:T(8,128)S(1)}, f32[8,8,128]{2,1,0:T(8,128)S(1)}, ...) custom-call(s32[256]{0:T(256)} %w_hbm.1, s32[128]{0:T(128)} %n_hbm.1, f32[1,64,128]{2,1,0:T(8,128)} %h_hbm.1, ...), custom_call_target="tpu_custom_call" | custom-call | tf_op jit(solution)/shard_map/gather/pallas_call | solution.py:352
  17.7 3.3 %invert.1 = (f32[8,8,64,128]{3,2,1,0:T(8,128)S(1)}, f32[8,8,64,128]{3,2,1,0:T(8,128)S(1)}, f32[8,8,64,128]{3,2,1,0:T(8,128)S(1)}, f32[8,8,64,128]{3,2,1,0:T(8,128)S(1)}) custom-call(f32[8,8,64,128]{3,2,1,0:T(8,128)S(1)} %get-tuple-element.18.e_in_real, ...), custom_call_target="tpu_custom_call", output_to_operand_aliasing={{0}: (0, {}), {1}: (1, {})} | custom-call | tf_op jit(solution)/shard_map/invert/pallas_call | solution.py:424
  21.0 16.4 %leave.1 = f32[16,2,128]{2,1,0:T(2,128)S(1)} custom-call(f32[8,64,128]{2,1,0:T(8,128)S(1)} %get-tuple-element.15.g_ref, f32[8,8,128]{2,1,0:T(8,128)S(1)} %get-tuple-element.16.ur_ref, f32[8,8,128]{2,1,0:T(8,128)S(1)} %get-tuple-element.17.ui_ref, f32[8,8,64,128]{3,2,1,0:T(8,128)S(1)} %get-tuple-element.21.er_ref, ...), custom_call_target="tpu_custom_call" | custom-call | tf_op jit(solution)/shard_map/leave/pallas_call | solution.py:523
  37.4 0.2 reshape.6
  37.7 0.7 %copy.10 = f32[16,256]{1,0:T(8,128)} copy(f32[16,256]{0,1:T(8,128)S(1)} %bitcast.3) | data formatting | bytes 32768 | tf_op jit(solution)/shard_map/reshape | solution.py:551
  (1 shorter events, 0.0 us)

commit v9 on v8

--- a/solution.py
+++ b/solution.py
@@ -57,7 +57,7 @@
     )
 
 
-Z_ORDER = (4, 3, 5, 2, 6, 1, 7)
+Z_ORDER = (1, 7, 4, 3, 5, 2, 6)
 SLOT_DX = (0, 1, 3, 2)
 
 
@@ -201,6 +201,9 @@
         hcol[p] = diagonal_columns(real)
         hrow[p : p + 1] = diagonal_row(real)
 
+    await_greetings = greet(
+        [along_z(dz) for dz in Z_ORDER] + [along_x(dx) for dx in (2, 1, 3)] + [partner]
+    )
     first_rows = pl.ds(0, PER_FREQ)
     own_h, own_z, own_g = hall.at[0, 0], zall.at[first_rows], gall.at[first_rows]
     loads = [
@@ -211,9 +214,6 @@
     ]
     for load in loads:
         load.start()
-    await_greetings = greet(
-        [along_z(dz) for dz in Z_ORDER] + [along_x(dx) for dx in (2, 1, 3)] + [partner]
-    )
     for load in loads:
         load.wait()
     h = h_ref[...]
@@ -456,19 +456,25 @@
     quarter = lanes % NORB // (NORB // YS)
 
     def last_product(n, carry):
-        t_real = t_imag = jnp.zeros((NORB, WIDE), F32)
+        totals = [None, None]
         for p in range(PAIRS):
-            q_real, q_imag = eye + er_ref[n, p], ei_ref[n, p]
-            right = right_blocks(br_ref[n, p], bi_ref[n, p])
-            real, imag = combine(product3(left_rows(q_real, q_imag), right))
-            q_real, q_imag = q_real + real, q_imag + imag
+            x_real, x_imag = eye + br_ref[n, p], bi_ref[n, p]
             u_real, u_imag = ur_ref[p, pl.ds(n, 1)], ui_ref[p, pl.ds(n, 1)]
-            t_real = t_real + (q_real * u_real - q_imag * u_imag)
-            t_imag = t_imag + (q_real * u_imag + q_imag * u_real)
-        t_ref[n] = jnp.where(first, t_real + swap(t_real), t_imag + swap(t_imag))
+            x_real, x_imag = x_real * u_real - x_imag * u_imag, x_real * u_imag + x_imag * u_real
+            right = jnp.concatenate(
+                [jnp.where(first, x_real, swap(x_imag)), jnp.where(first, swap(x_real), x_imag)], 0
+            )
+            right = jnp.concatenate(halves(right), 1)
+            left = jnp.concatenate(left_rows(eye + er_ref[n, p], ei_ref[n, p]), 1)
+            out = dot(left, jnp.concatenate([right, right], 0))
+            totals[p % 2] = out if p < 2 else totals[p % 2] + out
+        total = totals[0] + totals[1]
+        total = total[:, :WIDE] + total[:, WIDE:]
+        turned = swap(total[NORB:])
+        t_ref[n] = total[:NORB] + jnp.where(first, -turned, turned)
         return carry
 
-    lax.fori_loop(0, N_LOCAL, last_product, 0, unroll=4)
+    lax.fori_loop(0, N_LOCAL, last_product, 0, unroll=2)
     for n_high in range(2):
         mixed = [None] * YS
         for n_low in range(4):

time: 38.3 us -> 38.8 us (1.013)
  Pallas kernels: 37.4 us -> 38.1 us
    pallas_call x1, Pallas kernels: 16.4 us -> 17.4 us  [leave(): pl.pallas_call(exit_kernel, name='leave', out_shape=jax.ShapeDtypeStruct(...]
    pallas_call x1, Pallas kernels: 3.29 us -> 2.48 us  [invert(): pl.pallas_call(power_kernel, name='invert', out_shape=(powers,) * 4, in_s...]
    pallas_call x1, Pallas kernels: 17.7 us -> 18.2 us  [gather(): pl.pallas_call(gather_kernel, name='gather', out_shape=(totals, powers, p...]
where the time goes in v9:
time: 38.8 us; the launch traced here: 39.1 us
  Pallas kernels  38.1 us (98%)
  local copies, waits for them, and re-layouts  0.95 us (2%)
    pallas_call x1, Pallas kernels, gather(): pl.pallas_call(gather_kernel, name='gather', out_shape=(totals, powers, p...  18.2 us
    pallas_call x1, Pallas kernels, leave(): pl.pallas_call(exit_kernel, name='leave', out_shape=jax.ShapeDtypeStruct(...  17.4 us
    pallas_call x1, Pallas kernels, invert(): pl.pallas_call(power_kernel, name='invert', out_shape=(powers,) * 4, in_s...  2.48 us

profile of v9, /device:TPU:1, one launch (start us, length us, event | category | flops | bytes accessed | tf_op | source)
XLA Modules:
  0.0 39.1 jit_solution(17734716911101711309)
XLA Ops:
  0.0 18.2 %gather.1 = (f32[8,64,128]{2,1,0:T(8,128)S(1)}, f32[8,8,64,128]{3,2,1,0:T(8,128)S(1)}, f32[8,8,64,128]{3,2,1,0:T(8,128)S(1)}, f32[8,8,128]{2,1,0:T(8,128)S(1)}, ...) custom-call(s32[256]{0:T(256)} %w_hbm.1, s32[128]{0:T(128)} %n_hbm.1, f32[1,64,128]{2,1,0:T(8,128)} %h_hbm.1, ...), custom_call_target="tpu_custom_call" | custom-call | tf_op jit(solution)/shard_map/gather/pallas_call | solution.py:352
  18.2 2.5 %invert.1 = (f32[8,8,64,128]{3,2,1,0:T(8,128)S(1)}, f32[8,8,64,128]{3,2,1,0:T(8,128)S(1)}, f32[8,8,64,128]{3,2,1,0:T(8,128)S(1)}, f32[8,8,64,128]{3,2,1,0:T(8,128)S(1)}) custom-call(f32[8,8,64,128]{3,2,1,0:T(8,128)S(1)} %get-tuple-element.18.e_in_real, ...), custom_call_target="tpu_custom_call", output_to_operand_aliasing={{0}: (0, {}), {1}: (1, {})} | custom-call | tf_op jit(solution)/shard_map/invert/pallas_call | solution.py:424
  20.7 17.4 %leave.1 = f32[16,2,128]{2,1,0:T(2,128)S(1)} custom-call(f32[8,64,128]{2,1,0:T(8,128)S(1)} %get-tuple-element.15.g_ref, f32[8,8,128]{2,1,0:T(8,128)S(1)} %get-tuple-element.16.ur_ref, f32[8,8,128]{2,1,0:T(8,128)S(1)} %get-tuple-element.17.ui_ref, f32[8,8,64,128]{3,2,1,0:T(8,128)S(1)} %get-tuple-element.21.er_ref, ...), custom_call_target="tpu_custom_call" | custom-call | tf_op jit(solution)/shard_map/leave/pallas_call | solution.py:529
  38.1 0.2 reshape.6
  38.4 0.7 %copy.10 = f32[16,256]{1,0:T(8,128)} copy(f32[16,256]{0,1:T(8,128)S(1)} %bitcast.3) | data formatting | bytes 32768 | tf_op jit(solution)/shard_map/reshape | solution.py:557
  (1 shorter events, 0.0 us)

commit v10 on v9

--- a/solution.py
+++ b/solution.py
@@ -383,10 +383,6 @@
 def power_kernel(e_in_real, e_in_imag, count_ref, er_ref, ei_ref, br_ref, bi_ref, sr_ref, si_ref, steps_ref):
     eye = lane_masks()[2].astype(F32)
 
-    def one_step(n):
-        for p in range(PAIRS):
-            br_ref[n, p] = bi_ref[n, p] = jnp.zeros((NORB, WIDE), F32)
-
     def squares(n, real_ref, imag_ref):
         for p in range(PAIRS):
             e_real, e_imag = er_ref[n, p], ei_ref[n, p]
@@ -406,11 +402,10 @@
             br_ref[n, p], bi_ref[n, p] = combine(product3(left_rows(s_real, s_imag), right))
 
     for n in range(N_LOCAL):
-        steps_ref[n] = jnp.max(count_ref[n : n + 1])
+        steps_ref[n] = count_ref[n, 0]
 
     def one_freq(n, carry):
         steps = steps_ref[n]
-        pl.when(steps < 1.5)(functools.partial(one_step, n))
         pl.when((steps > 1.5) & (steps < 2.5))(functools.partial(two_steps, n))
         pl.when(steps > 2.5)(functools.partial(three_steps, n))
         return carry
@@ -434,7 +429,7 @@
 
 
 def exit_kernel(
-    g_ref, ur_ref, ui_ref, er_ref, ei_ref, br_ref, bi_ref, q_ref, o_ref, t_ref, landed, rows_ref, as_, ar, bs, br
+    g_ref, ur_ref, ui_ref, count_ref, er_ref, ei_ref, br_ref, bi_ref, q_ref, o_ref, t_ref, landed, rows_ref, as_, ar, bs, br
 ):
     f = lax.axis_index("freq")
     y = lax.axis_index("kgrp")
@@ -456,9 +451,11 @@
     quarter = lanes % NORB // (NORB // YS)
 
     def last_product(n, carry):
+        several = count_ref[pl.ds(n, 1)] > 1.5
         totals = [None, None]
         for p in range(PAIRS):
-            x_real, x_imag = eye + br_ref[n, p], bi_ref[n, p]
+            x_real = jnp.where(several, eye + br_ref[n, p], eye)
+            x_imag = jnp.where(several, bi_ref[n, p], 0.0)
             u_real, u_imag = ur_ref[p, pl.ds(n, 1)], ui_ref[p, pl.ds(n, 1)]
             x_real, x_imag = x_real * u_real - x_imag * u_imag, x_real * u_imag + x_imag * u_real
             right = jnp.concatenate(
@@ -530,7 +527,7 @@
         exit_kernel,
         name="leave",
         out_shape=jax.ShapeDtypeStruct((LINE, 2, WIDE), F32),
-        in_specs=[vmem()] * 7,
+        in_specs=[vmem()] * 8,
         out_specs=vmem(),
         scratch_shapes=[
             pltpu.VMEM((XS, YS, 2, LINE, WIDE), F32),
@@ -552,7 +549,7 @@
     g_all, e_real, e_imag, u_real, u_imag, steps = gather(
         weights, counts, hamiltonian, self_energy, guess_factor
     )
-    arrived = leave(g_all, u_real, u_imag, *invert(e_real, e_imag, steps))
+    arrived = leave(g_all, u_real, u_imag, steps, *invert(e_real, e_imag, steps))
     pieces = arrived.reshape(LINE, 2, 2, 2, 2, NORB // YS)
     return pieces.transpose(5, 2, 1, 3, 0, 4).reshape(NORB // YS, 2 * FREQ)
 

time: 38.8 us -> 38.1 us (0.982)
  Pallas kernels: 38.1 us -> 37.2 us
    pallas_call x1, Pallas kernels: 17.4 us -> 16.4 us  [leave(): pl.pallas_call(exit_kernel, name='leave', out_shape=jax.ShapeDtypeStruct(...]
where the time goes in v10:
time: 38.1 us; the launch traced here: 38.2 us
  Pallas kernels  37.2 us (98%)
  local copies, waits for them, and re-layouts  0.95 us (2%)
    pallas_call x1, Pallas kernels, gather(): pl.pallas_call(gather_kernel, name='gather', out_shape=(totals, powers, p...  18.2 us
    pallas_call x1, Pallas kernels, leave(): pl.pallas_call(exit_kernel, name='leave', out_shape=jax.ShapeDtypeStruct(...  16.4 us
    pallas_call x1, Pallas kernels, invert(): pl.pallas_call(power_kernel, name='invert', out_shape=(powers,) * 4, in_s...  2.61 us

profile of v10, /device:TPU:1, one launch (start us, length us, event | category | flops | bytes accessed | tf_op | source)
XLA Modules:
  0.0 38.2 jit_solution(11312464112311207917)
XLA Ops:
  0.0 18.2 %gather.1 = (f32[8,64,128]{2,1,0:T(8,128)S(1)}, f32[8,8,64,128]{3,2,1,0:T(8,128)S(1)}, f32[8,8,64,128]{3,2,1,0:T(8,128)S(1)}, f32[8,8,128]{2,1,0:T(8,128)S(1)}, ...) custom-call(s32[256]{0:T(256)} %w_hbm.1, s32[128]{0:T(128)} %n_hbm.1, f32[1,64,128]{2,1,0:T(8,128)} %h_hbm.1, ...), custom_call_target="tpu_custom_call" | custom-call | tf_op jit(solution)/shard_map/gather/pallas_call | solution.py:352
  18.2 2.6 %invert.1 = (f32[8,8,64,128]{3,2,1,0:T(8,128)S(1)}, f32[8,8,64,128]{3,2,1,0:T(8,128)S(1)}, f32[8,8,64,128]{3,2,1,0:T(8,128)S(1)}, f32[8,8,64,128]{3,2,1,0:T(8,128)S(1)}) custom-call(f32[8,8,64,128]{3,2,1,0:T(8,128)S(1)} %get-tuple-element.19.e_in_real, ...), custom_call_target="tpu_custom_call", output_to_operand_aliasing={{0}: (0, {}), {1}: (1, {})} | custom-call | tf_op jit(solution)/shard_map/invert/pallas_call | solution.py:419
  20.8 16.4 %leave.1 = f32[16,2,128]{2,1,0:T(2,128)S(1)} custom-call(f32[8,64,128]{2,1,0:T(8,128)S(1)} %get-tuple-element.15.g_ref, f32[8,8,128]{2,1,0:T(8,128)S(1)} %get-tuple-element.16.ur_ref, f32[8,8,128]{2,1,0:T(8,128)S(1)} %get-tuple-element.17.ui_ref, f32[8,128]{1,0:T(8,128)S(1)} %get-tuple-element.18.count_ref, f32[8,8,64,128]{3,2,1,0:T(8,128)S(1)} %get-tuple-element.21.er_ref, ...), custom_call_target="tpu_custom_call" | custom-call | tf_op jit(solution)/shard_map/leave/pallas_call | solution.py:526
  37.3 0.2 reshape.6
  37.6 0.7 %copy.10 = f32[16,256]{1,0:T(8,128)} copy(f32[16,256]{0,1:T(8,128)S(1)} %bitcast.3) | data formatting | bytes 32768 | tf_op jit(solution)/shard_map/reshape | solution.py:554
  (1 shorter events, 0.0 us)
